TPU v7x, 8 devices: a whole 2x2x1 slice. The times are simulated.
8 devices in a mesh: rep: 4 (over z, y, x), nodes: 2 (over core).
Axes of the slice: x: 2, y: 2, z: 1, core: 2. Of those that a mesh axis runs over, the one named last changes fastest.
Arguments:
- adjacency: bfloat16 [4, 4096, 16384], P(None, 'nodes', 'rep')
- features: bfloat16 [16384, 602], P(('rep', 'nodes'))
- w_one: float32 [602, 128], replicated
- w_two: float32 [128, 41], replicated
- labels: int32 [16384], P(('rep', 'nodes'))
- label_mask: int32 [16384], P(('rep', 'nodes'))
Outputs:
- output 1: float32 [], replicated
- output 2: float32 [602, 128], replicated
- output 3: float32 [128, 41], replicated
All inputs are finite; a program needn't handle non-finite values.
Results may differ from a plain program's by a relative error of at most 0.001.
Values are sent between devices in bfloat16 or wider.
A program may use at most 1 GiB of HBM per device.

v0:
```python
import jax
import jax.numpy as jnp
from jax import lax
from jax.sharding import PartitionSpec as P


def solution(mesh):
    all_axes = ("rep", "nodes")
    row_spec = P(("rep", "nodes"))

    def device_step(adj_blk, feat_blk, w_one, w_two, label_blk, mask_blk):
        n_class = w_two.shape[1]
        w_one_lo = w_one.astype(jnp.bfloat16)
        w_two_lo = w_two.astype(jnp.bfloat16)

        def spread(y_blk):
            gathered = lax.all_gather(y_blk, "nodes", axis=0, tiled=True)
            part_sum = lax.dot_general(adj_blk, gathered, (((2,), (0,)), ((), ())), preferred_element_type=jnp.float32)
            return lax.psum_scatter(part_sum, "rep", scatter_dimension=0, tiled=False)

        def collect(g_blk):
            gathered = lax.all_gather(g_blk, "rep", axis=0)
            part_sum = lax.dot_general(adj_blk, gathered, (((0, 1), (0, 1)), ((), ())), preferred_element_type=jnp.float32)
            return lax.psum_scatter(part_sum, "nodes", scatter_dimension=0, tiled=True)

        y_one = jnp.dot(feat_blk, w_one_lo, preferred_element_type=jnp.float32).astype(jnp.bfloat16)
        z_one = spread(y_one)
        h_one = jnp.maximum(z_one, 0.0).astype(jnp.bfloat16)
        y_two = jnp.dot(h_one, w_two_lo, preferred_element_type=jnp.float32).astype(jnp.bfloat16)
        z_two = spread(y_two)
        weights = mask_blk.astype(jnp.float32)
        log_probs = jax.nn.log_softmax(z_two, axis=-1)
        one_hot = (label_blk[:, None] == jnp.arange(n_class)[None, :]).astype(jnp.float32)
        local_sums = jnp.stack([jnp.sum(weights), -jnp.sum(weights * jnp.sum(one_hot * log_probs, axis=-1))])
        global_sums = lax.psum(local_sums, all_axes)
        label_count = global_sums[0]
        loss_value = global_sums[1] / label_count
        g_two = ((jnp.exp(log_probs) - one_hot) * (weights / label_count)[:, None]).astype(jnp.bfloat16)
        dy_two = collect(g_two).astype(jnp.bfloat16)
        dw_two = lax.psum(lax.dot_general(h_one, dy_two, (((0,), (0,)), ((), ())), preferred_element_type=jnp.float32), all_axes)
        dh_one = lax.dot_general(dy_two, w_two_lo, (((1,), (1,)), ((), ())), preferred_element_type=jnp.float32)
        g_one = jnp.where(z_one > 0.0, dh_one, 0.0).astype(jnp.bfloat16)
        dy_one = collect(g_one).astype(jnp.bfloat16)
        dw_one = lax.psum(lax.dot_general(feat_blk, dy_one, (((0,), (0,)), ((), ())), preferred_element_type=jnp.float32), all_axes)
        return loss_value, dw_one, dw_two

    return jax.shard_map(device_step, mesh=mesh, in_specs=(P(None, "nodes", "rep"), row_spec, P(), P(), row_spec, row_spec), out_specs=(P(), P(), P()), check_vma=False)
```

profile of v0, /device:TPU:0, one launch (start us, length us, event | category | flops | bytes accessed | tf_op | source)
XLA Modules:
  0.0 359.3 jit_solution(1124366052219068524)
XLA Ops:
  7.2 0.0 copy-start
  7.2 0.0 all-gather.4.cloned.1.call-start
  7.2 1.6 copy-done
  8.9 2.4 convolution_convert_fusion
  11.3 0.0 all-gather.4.cloned.1.call-update
  11.3 0.0 reduce-scatter.13.cloned.1.call-start
  11.3 9.0 %all-gather.4.cloned.1.call-done = bf16[4096,128]{0,1:T(8,128)(2,1)} async-done(((bf16[2048,128]{0,1:T(8,128)(2,1)}), bf16[4096,128]{0,1:T(8,128)(2,1)}) %all-gather.4.cloned.1.call-update) | async-done | bytes 1048592 | tf_op jit(solution)/shard_map/all_gather | solution.py:17
  20.4 32.1 %convolution_bitcast_fusion.2 = f32[4,2048,128]{1,2,0:T(8,128)} fusion(bf16[4,2048,4096]{2,1,0:T(8,128)(2,1)} %param.6, bf16[4096,128]{0,1:T(8,128)(2,1)} %all-gather.4.cloned.1.call-done), kind=kOutput, calls=%fused_computation.2 | convolution fusion | flops 8589934592 | bytes 72351744 | tf_op jit(solution)/shard_map/dot_general | solution.py:18
  52.5 0.0 reduce-scatter.13.cloned.1.call-update
  52.5 0.0 reduce-scatter.15.cloned.1.call-start
  52.6 48.1 %reduce-scatter.13.cloned.1.call-done = f32[1,2048,128]{1,2,0:T(8,128)} async-done(((f32[4,2048,128]{1,2,0:T(8,128)}), f32[1,2048,128]{1,2,0:T(8,128)}) %reduce-scatter.13.cloned.1.call-update) | async-done | bytes 1048592
  100.7 1.6 copy.10
  102.2 1.0 convolution_convert_fusion.1
  103.3 2.0 all_gather.17
  105.3 29.5 %convolution_bitcast_fusion.3 = f32[4,2048,41]{1,2,0:T(8,128)} fusion(bf16[4,2048,4096]{2,1,0:T(8,128)(2,1)} %param.6, bf16[4096,41]{0,1:T(8,128)(2,1)} %all_gather.17), kind=kOutput, calls=%fused_computation.3 | convolution fusion | flops 2751463424 | bytes 68788224 | tf_op jit(solution)/shard_map/dot_general | solution.py:18
  134.8 0.0 reduce-scatter.15.cloned.1.call-update
  134.9 0.0 reduce-scatter.9.cloned.1.call-start
  134.9 25.6 %reduce-scatter.15.cloned.1.call-done = f32[1,2048,41]{1,2,0:T(8,128)} async-done(((f32[4,2048,41]{1,2,0:T(8,128)}), f32[1,2048,41]{1,2,0:T(8,128)}) %reduce-scatter.15.cloned.1.call-update) | async-done | bytes 335888
  160.5 1.0 reduce_max.10
  161.6 1.1 exponential_reduce_fusion
  162.7 1.1 select_reduce_fusion
  163.7 1.3 convert_reduce_fusion
  165.7 1.2 pad_maximum_fusion
  166.9 22.4 %psum.21 = f32[2]{0:T(128)} all-reduce(f32[2]{0:T(128)} %pad_maximum_fusion), channel_id=1, replica_groups=mesh['rep'=4,'nodes'=2] {'rep','nodes'}, use_global_device_ids=true, to_apply=%region_7.8 | all-reduce | flops 2 | bytes 16 | tf_op jit(solution)/shard_map/psum | solution.py:35
  189.4 1.3 fusion.15
  190.7 1.3 convert_divide_fusion
  192.0 1.1 multiply_convert_fusion
  193.1 12.6 %all_gather.18 = bf16[4,2048,41]{1,2,0:T(8,128)(2,1)} all-gather(bf16[1,2048,41]{1,2,0:T(8,128)(2,1)S(1)} %multiply_convert_fusion), channel_id=1, replica_groups=mesh['rep'=4,'nodes'=2] {'rep'}, dimensions={0}, use_global_device_ids=true | all-gather | bytes 839680 | tf_op jit(solution)/shard_map/all_gather | solution.py:22
  205.8 25.3 %convolution_bitcast_fusion.1 = f32[4096,41]{0,1:T(8,128)} fusion(bf16[4,2048,41]{1,2,0:T(8,128)(2,1)} %all_gather.18, bf16[4,2048,4096]{2,1,0:T(8,128)(2,1)} %param.6), kind=kOutput, calls=%fused_computation.1 | convolution fusion | flops 2751463424 | bytes 68452352 | tf_op jit(solution)/shard_map/dot_general | solution.py:23
  231.1 0.0 reduce-scatter.9.cloned.1.call-update
  231.1 0.0 all-gather.6.cloned.1.call-start
  231.2 5.7 %reduce-scatter.9.cloned.1.call-done = f32[2048,41]{0,1:T(8,128)} async-done(((f32[4096,41]{0,1:T(8,128)}), f32[2048,41]{0,1:T(8,128)}) %reduce-scatter.9.cloned.1.call-update) | async-done | bytes 335888 | tf_op jit(solution)/shard_map/reduce_scatter | solution.py:24
  236.8 2.1 fusion
  238.9 0.0 all-gather.6.cloned.1.call-update
  239.0 0.2 reduce-scatter.11.cloned.1.call-start
  239.2 30.4 %all-gather.6.cloned.1.call-done = bf16[8192,128]{1,0:T(8,128)(2,1)} async-done(((bf16[2048,128]{1,0:T(8,128)(2,1)}), bf16[8192,128]{1,0:T(8,128)(2,1)}) %all-gather.6.cloned.1.call-update) | async-done | bytes 2097168 | tf_op jit(solution)/shard_map/all_gather | solution.py:22
  269.6 25.8 %convolution_bitcast_fusion = f32[4096,128]{0,1:T(8,128)} fusion(bf16[4,2048,128]{2,1,0:T(8,128)(2,1)} %bitcast.46, bf16[4,2048,4096]{2,1,0:T(8,128)(2,1)} %param.6), kind=kOutput, calls=%fused_computation | convolution fusion | flops 8589934592 | bytes 71303168 | tf_op jit(solution)/shard_map/dot_general | solution.py:23
  295.4 0.0 reduce-scatter.11.cloned.1.call-update
  295.4 0.0 all-reduce.4.cloned.1.call-start
  296.8 5.3 %reduce-scatter.11.cloned.1.call-done = f32[2048,128]{0,1:T(8,128)} async-done(((f32[4096,128]{0,1:T(8,128)}), f32[2048,128]{0,1:T(8,128)}) %reduce-scatter.11.cloned.1.call-update) | async-done | bytes 1048592 | tf_op jit(solution)/shard_map/reduce_scatter | solution.py:24
  302.1 2.8 convolution_bitcast_fusion.4
  304.8 0.0 all-reduce.4.cloned.1.call-update
  304.8 1.8 fusion.5
  306.7 24.0 %psum.23 = f32[128,41]{0,1:T(8,128)} all-reduce(f32[128,41]{0,1:T(8,128)} %fusion.5), channel_id=1, replica_groups=mesh['rep'=4,'nodes'=2] {'rep','nodes'}, use_global_device_ids=true, to_apply=%region_11.12 | all-reduce | flops 5248 | bytes 41984 | tf_op jit(solution)/shard_map/psum | solution.py:40
  330.6 19.0 %all-reduce.4.cloned.1.call-done = f32[602,128]{1,0:T(8,128)} async-done(((f32[602,128]{1,0:T(8,128)}), f32[602,128]{1,0:T(8,128)}) %all-reduce.4.cloned.1.call-update) | async-done | bytes 308240 | tf_op jit(solution)/shard_map/psum | solution.py:44
  349.6 1.7 copy.13
  (1 shorter events, 0.0 us)
Async XLA Ops:
  7.2 1.7 copy-start
  7.2 13.2 %all-gather.4.cloned.1.call-start = ((), (), s32[]{:S(2)}) async-start(), calls=%async_computation.4 | async-start | bytes 1572864 | tf_op jit(solution)/shard_map/all_gather | solution.py:17
  11.3 89.4 %reduce-scatter.13.cloned.1.call-start = ((), (), s32[]{:S(2)}) async-start(), calls=%async_computation.9 | async-start | bytes 5242880
  52.5 108.0 %reduce-scatter.15.cloned.1.call-start = ((), (), s32[]{:S(2)}) async-start(), calls=%async_computation.10 | async-start | bytes 1966080
  134.9 101.9 %reduce-scatter.9.cloned.1.call-start = ((), (), s32[]{:S(2)}) async-start(), calls=%async_computation.5 | async-start | bytes 1179648 | tf_op jit(solution)/shard_map/reduce_scatter | solution.py:24
  231.1 38.5 %all-gather.6.cloned.1.call-start = ((), (), s32[]{:S(2)}) async-start(), calls=%async_computation.8 | async-start | bytes 2621440 | tf_op jit(solution)/shard_map/all_gather | solution.py:22
  239.0 63.1 %reduce-scatter.11.cloned.1.call-start = ((), (), s32[]{:S(2)}) async-start(), calls=%async_computation.6 | async-start | bytes 3145728 | tf_op jit(solution)/shard_map/reduce_scatter | solution.py:24
  295.4 54.2 %all-reduce.4.cloned.1.call-start = ((), (), s32[]{:S(2)}) async-start(), calls=%async_computation.7 | async-start | bytes 622592 | tf_op jit(solution)/shard_map/psum | solution.py:44
Sparse Core Ops, SparseCore 0:
  11.4 8.9 all-gather.3
  52.7 47.9 reduce-scatter.12
  135.0 25.4 reduce-scatter.14
  231.2 5.5 reduce-scatter.8
  239.1 30.4 all-gather.5
  295.5 6.4 reduce-scatter.10
  305.7 43.8 all-reduce.3
where the time goes:
time: 360 us; the launch traced here: 359 us
  waiting for transfers between devices  143 us (40%)
  matrix products  123 us (34%)
  blocking collectives  61 us (17%)
  between operations  17.3 us (5%)
  other arithmetic  8.19 us (2%)
  local copies, waits for them, and re-layouts  6.23 us (2%)
    unnamed x9, waiting for transfers between devices  73.8 us
    dot_general x2, matrix products, spread(): lax.dot_general(adj_blk, gathered, (((2,), (0,)), ((), ())), preferred_el...  61.7 us
    dot_general x2, matrix products, collect(): lax.dot_general(adj_blk, gathered, (((0, 1), (0, 1)), ((), ())), preferre...  51.1 us
    all_gather x1, waiting for transfers between devices, collect(): gathered = lax.all_gather(g_blk, 'rep', axis=0)  30.4 us
    psum x1, blocking collectives, device_step(): lax.psum(lax.dot_general(h_one, dy_two, (((0,), (0,)), ((), ())), preferr...  24 us
    psum x1, blocking collectives, device_step(): global_sums = lax.psum(local_sums, all_axes)  22.4 us
    psum x1, waiting for transfers between devices, device_step(): lax.psum(lax.dot_general(feat_blk, dy_one, (((0,), (0,)), ((), ())), pref...  19 us
    all_gather x1, blocking collectives, collect(): gathered = lax.all_gather(g_blk, 'rep', axis=0)  12.6 us
  transfers between devices with their start and end apart: 7, of which 7 were waited for; matrix products, arithmetic and copies ran while one was open for 1% of the time, Pallas kernels for 0%

commit v1 on v0

v1 whole, which is shorter than its diff:
```python
import jax
import jax.numpy as jnp
from jax import lax
from jax.experimental import pallas as pl
from jax.experimental.pallas import tpu as pltpu
from jax.sharding import PartitionSpec as P

BF = jnp.bfloat16
F32 = jnp.float32
MESH = pl.DeviceIdType.MESH

CH = 256
NCH = 8
CP = 48
L2, L3, L4 = 2, 4, 5
M1, M2, M3 = 1, 2, 3
N1 = 1


def mm(a, b, ca=1, cb=0):
    return lax.dot_general(a, b, (((ca,), (cb,)), ((), ())), preferred_element_type=F32)


def kernel(
    n_class, adj, feat, w1, w2, lab, loss_o, dw1_o, dw2_o,
    a_s, x_s, w2n, w2t, y1, p1, p1r1, p1r2, h1t, y2, zacc, zs, zr1, zr2, g2, dacc, drec, g1, eacc, erec,
    cnt, cntr, f2, f2r, fw, fr0, fs, fr1, fr2, fo, lossv,
    a_sem, x_sem, y1_ss, y1_rs, p1_ss, p1_rs, y2_ss, y2_rs, z_ss, z_rs, g2_ss, g2_rs, g1_ss, g1_rs,
    d_ss, d_rs, c_ss, c_rs, f2_ss, f2_rs, fw_ss, fw_rs,
):
    r = lax.axis_index("rep")
    i = lax.axis_index("nodes")
    nbx = r + 1 - 2 * (r % 2)
    nby = (r + 2) % 4
    r0, r1 = r % 2, r // 2
    other = 1 - i

    def near(e):
        return nbx * (1 - e) + nby * e

    def far(e):
        return nby * (1 - e) + nbx * e

    def place(a, e):
        d0 = (r0 + a % 2) % 2
        d1 = (r1 + a // 2) % 2
        return 3 * (1 - d0) * (1 - d1) + d0 * (1 - d1) * (1 + e) + (1 - d0) * d1 * (2 - e)

    def remote(src, dst, ss, rs, rep, core):
        return pltpu.make_async_remote_copy(
            src_ref=src, dst_ref=dst, send_sem=ss, recv_sem=rs, device_id=(rep, core), device_id_type=MESH
        )

    def rows_copy(chunk, slot):
        return pltpu.make_async_copy(
            adj.at[:, pl.ds(pl.multiple_of(chunk * CH, CH), CH), :], a_s.at[slot], a_sem.at[slot]
        )

    def cols_start(k, slot):
        @pl.loop(0, NCH)
        def _(g):
            for core in range(2):
                pltpu.make_async_copy(
                    adj.at[:, pl.ds(pl.multiple_of(g * CH, CH), CH), pl.ds(pl.multiple_of(core * 2048 + k * CH, CH), CH)],
                    a_s.at[slot, :, :, pl.ds(pl.multiple_of(g * 2 * CH + core * CH, CH), CH)],
                    a_sem.at[slot],
                ).start()

    x_copy = pltpu.make_async_copy(feat, x_s, x_sem)
    x_copy.start()
    rows_copy(0, 0).start()
    rows_copy(1, 1).start()
    cols_start(0, 2)
    cols_start(1, 3)

    barrier = pltpu.get_barrier_semaphore()
    pl.semaphore_signal(barrier, inc=1, device_id=(nbx, i), device_id_type=MESH)
    pl.semaphore_signal(barrier, inc=1, device_id=(nby, i), device_id_type=MESH)
    pl.semaphore_signal(barrier, inc=1, device_id=(r, other), device_id_type=MESH)

    w2n[...] = jnp.zeros_like(w2n)
    w2n[:, 0:n_class] = w2[...]
    w2t[...] = jnp.transpose(w2n[...], (1, 0)).astype(BF)
    zacc[...] = jnp.zeros_like(zacc)
    dacc[...] = jnp.zeros_like(dacc)
    eacc[...] = jnp.zeros_like(eacc)
    lossv[...] = jnp.zeros_like(lossv)
    f2[0] = jnp.zeros_like(f2[0])
    mask_all = jnp.where(lab[...] >= 0, 1.0, 0.0).astype(F32)
    total = jnp.sum(jnp.sum(mask_all, axis=0, keepdims=True), axis=1, keepdims=True)
    cnt[0] = jnp.broadcast_to(total, (8, 128))
    w1b = w1[...].astype(BF)
    pl.semaphore_wait(barrier, 3)

    def cnt_copy(n):
        rep = (nbx, nby, r)[n]
        core = (i, i, other)[n]
        return remote(cnt.at[n], cntr.at[n], c_ss.at[n], c_rs.at[n], rep, core)

    cnt_copy(0).start()
    x_copy.wait()

    def y1_copy(b):
        part = y1.at[i, pl.ds(pl.multiple_of(b * 512, 512), 512), :]
        return remote(part, part, y1_ss.at[b], y1_rs.at[b], r, other)

    def y1_recv(b):
        part = y1.at[other, pl.ds(pl.multiple_of(b * 512, 512), 512), :]
        return remote(part, part, y1_ss.at[b], y1_rs.at[b], r, other)

    @pl.loop(0, 4)
    def _(b):
        rows = pl.ds(pl.multiple_of(b * 512, 512), 512)
        y1[i, rows, :] = mm(x_s[rows, :], w1b).astype(BF)
        y1_copy(b).start()

    cnt_copy(0).wait_recv()
    cnt[1] = cnt[0] + cntr[0]
    cnt_copy(1).start()

    @pl.loop(0, 4)
    def _(b):
        y1_recv(b).wait_recv()

    def p1_first(c, e):
        return remote(p1.at[c, pl.ds(0, 2)], p1r1.at[c], p1_ss.at[0, c], p1_rs.at[0, c], near(e), i)

    def p1_second(c, e):
        return remote(p1.at[c, 2], p1r2.at[c], p1_ss.at[1, c], p1_rs.at[1, c], far(e), i)

    def y2_copy(c):
        return remote(y2.at[c, i], y2.at[c, i], y2_ss.at[c], y2_rs.at[c], r, other)

    def y2_recv(c):
        return remote(y2.at[c, other], y2.at[c, other], y2_ss.at[c], y2_rs.at[c], r, other)

    def z_part(lhs, slot, g):
        rhs = a_s[slot, :, :, pl.ds(pl.multiple_of(g * 2 * CH, 2 * CH), 2 * CH)].reshape(4 * CH, 2 * CH)
        return mm(lhs, rhs, 1, 1)

    def pass2_lhs(k):
        return jnp.concatenate([y2[k, 0], y2[k, 1]], axis=1)

    @pl.loop(0, NCH - 1 + L4)
    def _(t):
        @pl.when(t < NCH)
        def _():
            c = t
            e = c % 2
            rows_copy(c, e).wait()
            res = mm(a_s[e].reshape(4 * CH, 4096), y1[...].reshape(4096, 128))
            for a in range(4):
                p1[c, place(a, e)] = res[a * CH:(a + 1) * CH]
            p1_first(c, e).start()

            @pl.when(c + 2 < NCH)
            def _():
                rows_copy(c + 2, e).start()

        @pl.when(jnp.logical_and(t >= L2, t < NCH + L2))
        def _():
            c = t - L2
            e = c % 2
            p1_first(c, e).wait_recv()
            p1[c, 2] = p1[c, 2] + p1r1[c, 0]
            p1_second(c, e).start()
            p1[c, 3] = p1[c, 3] + p1r1[c, 1]

        @pl.when(jnp.logical_and(t >= L3, t < NCH + L3))
        def _():
            c = t - L3
            e = c % 2
            p1_second(c, e).wait_recv()
            h = jnp.maximum(p1[c, 3] + p1r2[c], 0.0)
            ht = jnp.transpose(h, (1, 0)).astype(BF)
            h1t[c] = ht
            y2[c, i] = mm(w2t[...], ht).astype(BF)
            y2_copy(c).start()

        @pl.when(t >= L4)
        def _():
            k = t - L4
            slot = 2 + k % 2
            y2_recv(k).wait_recv()
            rows_copy(0, slot).wait()
            lhs = pass2_lhs(k)

            @pl.loop(0, 2)
            def _(gg):
                for g4 in range(4):
                    g = gg * 4 + g4
                    zacc[g] = zacc[g] + z_part(lhs, slot, g)

            @pl.when(k + 2 < NCH)
            def _():
                cols_start(k + 2, slot)

            @pl.when(k + 2 == NCH)
            def _():
                rows_copy(0, 2).start()

    def z_first(q, e):
        return remote(zs.at[q, pl.ds(0, 2)], zr1.at[q], z_ss.at[0, q], z_rs.at[0, q], near(e), i)

    def z_second(q, e):
        return remote(zs.at[q, 2], zr2.at[q], z_ss.at[1, q], z_rs.at[1, q], far(e), i)

    def spread_first(buf, ss, rs, q, e):
        return remote(buf.at[q, 3], buf.at[q, 2], ss.at[0, q], rs.at[0, q], far(e), i)

    def spread_second(buf, ss, rs, q, e):
        return remote(buf.at[q, pl.ds(2, 2)], buf.at[q, pl.ds(0, 2)], ss.at[1, q], rs.at[1, q], near(e), i)

    y2_recv(NCH - 1).wait_recv()
    rows_copy(0, 3).wait()
    lhs_last = pass2_lhs(NCH - 1)

    @pl.loop(0, NCH)
    def _(q):
        g = (q + 6) % NCH
        e = q % 2
        z = zacc[g] + z_part(lhs_last, 3, g)
        for a in range(4):
            zs[q, place(a, e)] = z[:, a * CH:(a + 1) * CH]
        z_first(q, e).start()

    rows_copy(1, 3).start()
    cnt_copy(1).wait_recv()
    cnt[2] = cnt[1] + cntr[1]
    cnt_copy(2).start()
    cnt_copy(2).wait_recv()
    count = (cnt[2] + cntr[2])[0:1, 0:1]
    class_id = lax.broadcasted_iota(jnp.int32, (CP, CH), 0)

    def gathered(buf, q, e):
        return jnp.concatenate([buf[q, place(a, e)] for a in range(4)], axis=1)

    def half(core):
        return pl.ds(pl.multiple_of(core * 2048, 2048), 2048)

    def pair_copy(src, dst, n):
        return remote(src.at[:, half(other)], dst, d_ss.at[n], d_rs.at[n], r, other)

    @pl.loop(0, NCH + M3)
    def _(t):
        @pl.when(t < NCH)
        def _():
            q = t
            e = q % 2
            z_first(q, e).wait_recv()
            zs[q, 2] = zs[q, 2] + zr1[q, 0]
            z_second(q, e).start()
            zs[q, 3] = zs[q, 3] + zr1[q, 1]

        @pl.when(jnp.logical_and(t >= M1, t < NCH + M1))
        def _():
            q = t - M1
            e = q % 2
            z_second(q, e).wait_recv()
            z = jnp.where(class_id < n_class, zs[q, 3] + zr2[q], -1e30)
            top = jnp.max(z, axis=0, keepdims=True)
            shifted = z - top
            log_p = shifted - jnp.log(jnp.sum(jnp.exp(shifted), axis=0, keepdims=True))
            label = lab[pl.ds((q + 6) % NCH, 1), :]
            weight = jnp.where(label >= 0, 1.0, 0.0).astype(F32)
            hit = class_id == label
            lossv[...] = lossv[...] - weight * jnp.sum(jnp.where(hit, log_p, 0.0), axis=0, keepdims=True)
            prob = jnp.exp(log_p)
            g2[q, 3] = ((prob - jnp.where(hit, 1.0, 0.0)) * (weight / count)).astype(BF)
            spread_first(g2, g2_ss, g2_rs, q, e).start()

        @pl.when(jnp.logical_and(t >= M2, t < NCH + M2))
        def _():
            q = t - M2
            e = q % 2
            spread_first(g2, g2_ss, g2_rs, q, e).wait_recv()
            spread_second(g2, g2_ss, g2_rs, q, e).start()

        @pl.when(t >= M3)
        def _():
            q = t - M3
            e = q % 2
            slot = q % 4
            spread_second(g2, g2_ss, g2_rs, q, e).wait_recv()

            @pl.when(q >= 2)
            def _():
                rows_copy(0, slot).wait()

            lhs = gathered(g2, q, e)
            dacc[:, half(other)] += mm(lhs, a_s[slot, :, :, half(other)].reshape(4 * CH, 2048))

            @pl.when(q == NCH - 1)
            def _():
                pair_copy(dacc, drec, 0).start()

            dacc[:, half(i)] += mm(lhs, a_s[slot, :, :, half(i)].reshape(4 * CH, 2048))

            @pl.when(q < 4)
            def _():
                rows_copy((q + 10) % NCH, slot).start()

    pair_copy(dacc, drec, 0).wait_recv()

    def dy2_part(c):
        cols = pl.ds(pl.multiple_of(i * 2048 + c * CH, CH), CH)
        return (dacc[:, cols] + drec[:, pl.ds(pl.multiple_of(c * CH, CH), CH)]).astype(BF)

    w2b = w2n[...].astype(BF)

    @pl.loop(0, NCH)
    def _(q):
        c = (q + 2) % NCH
        dh = mm(w2b, dy2_part(c))
        g1[q, 3] = jnp.where(h1t[c].astype(F32) > 0.0, dh, 0.0).astype(BF)
        spread_first(g1, g1_ss, g1_rs, q, q % 2).start()

    @pl.loop(0, NCH)
    def _(c):
        f2[0, 0:128, 0:CP] += mm(h1t[c], dy2_part(c), 1, 1)

    f2[0, 128:136, :] = jnp.broadcast_to(jnp.sum(lossv[...], axis=1, keepdims=True), (8, 128))

    def f2_copy(n):
        rep = (nbx, nby, r)[n]
        core = (i, i, other)[n]
        return remote(f2.at[n], f2r.at[n], f2_ss.at[n], f2_rs.at[n], rep, core)

    f2_copy(0).start()

    @pl.loop(0, NCH + N1)
    def _(t):
        @pl.when(t < NCH)
        def _():
            q = t
            e = q % 2
            spread_first(g1, g1_ss, g1_rs, q, e).wait_recv()
            spread_second(g1, g1_ss, g1_rs, q, e).start()

        for n in range(2):
            @pl.when(t == 3 + 2 * n)
            def _():
                f2_copy(n).wait_recv()
                f2[n + 1] = f2[n] + f2r[n]
                f2_copy(n + 1).start()

        @pl.when(t >= N1)
        def _():
            q = t - N1
            e = q % 2
            slot = q % 4
            spread_second(g1, g1_ss, g1_rs, q, e).wait_recv()

            @pl.when(q >= 4)
            def _():
                rows_copy(0, slot).wait()

            lhs = gathered(g1, q, e)
            eacc[:, half(other)] += mm(lhs, a_s[slot, :, :, half(other)].reshape(4 * CH, 2048))

            @pl.when(q == NCH - 1)
            def _():
                pair_copy(eacc, erec, 1).start()

            eacc[:, half(i)] += mm(lhs, a_s[slot, :, :, half(i)].reshape(4 * CH, 2048))

            @pl.when(q < 4)
            def _():
                rows_copy((q + 6) % NCH, slot).start()

    f2_copy(2).wait_recv()
    pair_copy(eacc, erec, 1).wait_recv()
    dy1 = (eacc[:, half(i)] + erec[...]).astype(BF)
    n_in = dw1_o.shape[0]
    fw[...] = jnp.zeros_like(fw)
    fw[:, 0:n_in] = mm(dy1, x_s[...])
    fw_t = jnp.transpose(fw[...], (1, 0))
    fs[0, 0] = fw_t[0:320]
    fs[0, 1] = fw_t[320:640]

    def pair_half():
        return remote(fs.at[0, other], fr0, fw_ss.at[0], fw_rs.at[0], r, other)

    def quarter(n, h):
        rep = nbx * (1 - (n + h) % 2) + nby * ((n + h) % 2)
        return remote(
            fs.at[1 + n, 0, pl.ds(h * 160, 160)], fr1.at[n, pl.ds(h * 160, 160)],
            fw_ss.at[1 + 2 * n + h], fw_rs.at[1 + 2 * n + h], rep, i,
        )

    def back():
        return remote(fs.at[2, 1], fr2, fw_ss.at[5], fw_rs.at[5], r, other)

    pair_half().start()
    pair_half().wait_recv()
    fs[1, 0] = fs[0, i] + fr0[...]
    for h in range(2):
        quarter(0, h).start()
    for h in range(2):
        quarter(0, h).wait_recv()
        fs[2, 0, h * 160:(h + 1) * 160] = fs[1, 0, h * 160:(h + 1) * 160] + fr1[0, h * 160:(h + 1) * 160]
        quarter(1, h).start()
    for h in range(2):
        quarter(1, h).wait_recv()
    fs[2, 1] = fs[2, 0] + fr1[1]
    back().start()
    f_sum = f2[2] + f2r[2]
    dw2_o[...] = f_sum[0:128, 0:n_class]
    loss_o[...] = f_sum[128:129, 0:1] / count
    back().wait_recv()
    fo[i] = fs[2, 1]
    fo[other] = fr2[...]
    dw1_o[0:320] = fo[0]
    dw1_o[320:n_in] = fo[1, 0:n_in - 320]

    @pl.loop(0, 4)
    def _(b):
        y1_copy(b).wait_send()

    @pl.loop(0, NCH)
    def _(c):
        e = c % 2
        p1_first(c, e).wait_send()
        p1_second(c, e).wait_send()
        y2_copy(c).wait_send()
        z_first(c, e).wait_send()
        z_second(c, e).wait_send()
        spread_first(g2, g2_ss, g2_rs, c, e).wait_send()
        spread_second(g2, g2_ss, g2_rs, c, e).wait_send()
        spread_first(g1, g1_ss, g1_rs, c, e).wait_send()
        spread_second(g1, g1_ss, g1_rs, c, e).wait_send()

    for n in range(3):
        cnt_copy(n).wait_send()
        f2_copy(n).wait_send()
    pair_copy(dacc, drec, 0).wait_send()
    pair_copy(eacc, erec, 1).wait_send()
    pair_half().wait_send()
    for n in range(2):
        for h in range(2):
            quarter(n, h).wait_send()
    back().wait_send()


def solution(mesh):
    def device_step(adj, feat, w1, w2, labels, mask):
        n_in, n_hid = w1.shape
        n_class = w2.shape[1]
        lab = jnp.where(mask > 0, labels, -1).reshape(NCH, CH)
        vmem = pl.BlockSpec(memory_space=pltpu.VMEM)
        hbm = pl.BlockSpec(memory_space=pl.ANY)
        dma = pltpu.SemaphoreType.DMA

        def body(*refs):
            kernel(n_class, *refs)

        loss, dw1, dw2 = pl.pallas_call(
            body,
            out_shape=(
                jax.ShapeDtypeStruct((1, 1), F32),
                jax.ShapeDtypeStruct((n_in, n_hid), F32),
                jax.ShapeDtypeStruct((n_hid, n_class), F32),
            ),
            in_specs=[hbm, hbm, vmem, vmem, vmem],
            out_specs=(vmem, vmem, vmem),
            scratch_shapes=[
                pltpu.VMEM((4, 4, CH, 4096), BF),
                pltpu.VMEM((2048, n_in), BF),
                pltpu.VMEM((128, CP), F32),
                pltpu.VMEM((CP, 128), BF),
                pltpu.VMEM((2, 2048, 128), BF),
                pltpu.VMEM((NCH, 4, CH, 128), F32),
                pltpu.VMEM((NCH, 2, CH, 128), F32),
                pltpu.VMEM((NCH, CH, 128), F32),
                pltpu.VMEM((NCH, 128, CH), BF),
                pltpu.VMEM((NCH, 2, CP, CH), BF),
                pltpu.VMEM((NCH, CP, 4 * CH), F32),
                pltpu.VMEM((NCH, 4, CP, CH), F32),
                pltpu.VMEM((NCH, 2, CP, CH), F32),
                pltpu.VMEM((NCH, CP, CH), F32),
                pltpu.VMEM((NCH, 4, CP, CH), BF),
                pltpu.VMEM((CP, 4096), F32),
                pltpu.VMEM((CP, 2048), F32),
                pltpu.VMEM((NCH, 4, 128, CH), BF),
                pltpu.VMEM((128, 4096), F32),
                pltpu.VMEM((128, 2048), F32),
                pltpu.VMEM((3, 8, 128), F32),
                pltpu.VMEM((3, 8, 128), F32),
                pltpu.VMEM((3, 136, 128), F32),
                pltpu.VMEM((3, 136, 128), F32),
                pltpu.VMEM((128, 640), F32),
                pltpu.VMEM((320, 128), F32),
                pltpu.VMEM((3, 2, 320, 128), F32),
                pltpu.VMEM((2, 320, 128), F32),
                pltpu.VMEM((320, 128), F32),
                pltpu.VMEM((2, 320, 128), F32),
                pltpu.VMEM((1, CH), F32),
                dma((4,)), dma(()),
                dma((4,)), dma((4,)),
                dma((2, NCH)), dma((2, NCH)),
                dma((NCH,)), dma((NCH,)),
                dma((2, NCH)), dma((2, NCH)),
                dma((2, NCH)), dma((2, NCH)),
                dma((2, NCH)), dma((2, NCH)),
                dma((2,)), dma((2,)),
                dma((3,)), dma((3,)),
                dma((3,)), dma((3,)),
                dma((6,)), dma((6,)),
            ],
            compiler_params=pltpu.CompilerParams(
                collective_id=0, has_side_effects=True, vmem_limit_bytes=67043328
            ),
        )(adj, feat, w1, w2, lab)
        return loss.reshape(()), dw1, dw2

    row_spec = P(("rep", "nodes"))
    return jax.shard_map(
        device_step,
        mesh=mesh,
        in_specs=(P(None, "nodes", "rep"), row_spec, P(), P(), row_spec, row_spec),
        out_specs=(P(), P(), P()),
        check_vma=False,
    )
```

time: 360 us -> 160 us (0.44)
  Pallas kernels: 0 us -> 147 us
  waiting for transfers between devices: 143 us -> 0 us
  matrix products: 123 us -> 0 us
  blocking collectives: 61 us -> 0 us
  between operations: 17.3 us -> 2.4 us
  other arithmetic: 8.19 us -> 0.72 us
    pallas_call x0 -> x1, Pallas kernels: none -> 147 us  [device_step(): pl.pallas_call(body, out_shape=(jax.ShapeDtypeStruct((1, 1), F32), jax.Sh...]
    dot_general x9 -> x0, matrix products: 123 us -> none  [the longest x2 61.7 us: spread(): lax.dot_general(adj_blk, gathered, (((2,), (0,)), ((), ())), preferred_el...]
    unnamed x9 -> x0, waiting for transfers between devices: 73.8 us -> none
    psum x2 -> x0, blocking collectives: 46.4 us -> none  [the longest x1 24 us: device_step(): lax.psum(lax.dot_general(h_one, dy_two, (((0,), (0,)), ((), ())), preferr...]
    all_gather x2 -> x0, waiting for transfers between devices: 39.4 us -> none  [the longest x1 30.4 us: collect(): gathered = lax.all_gather(g_blk, 'rep', axis=0)]
    psum x1 -> x0, waiting for transfers between devices: 19 us -> none  [device_step(): lax.psum(lax.dot_general(feat_blk, dy_one, (((0,), (0,)), ((), ())), pref...]
    all_gather x2 -> x0, blocking collectives: 14.7 us -> none  [the longest x1 12.6 us: collect(): gathered = lax.all_gather(g_blk, 'rep', axis=0)]
    reduce_scatter x2 -> x0, waiting for transfers between devices: 10.9 us -> none  [collect(): return lax.psum_scatter(part_sum, 'nodes', scatter_dimension=0, tiled=True)]
  transfers between devices with their start and end apart: 7 -> 0, of which waited for: 7 -> 0; matrix products, arithmetic and copies ran while one was open for 1% -> 0% of each run, Pallas kernels for 0% -> 0%
where the time goes in v1:
time: 160 us; the launch traced here: 159 us
  Pallas kernels  147 us (92%)
  local copies, waits for them, and re-layouts  9.67 us (6%)
  between operations  2.4 us (2%)
    pallas_call x1, Pallas kernels, device_step(): pl.pallas_call(body, out_shape=(jax.ShapeDtypeStruct((1, 1), F32), jax.Sh...  147 us
    unnamed x4, local copies, waits for them, and re-layouts  9.07 us

profile of v1, /device:TPU:0, one launch (start us, length us, event | category | flops | bytes accessed | tf_op | source)
XLA Modules:
  0.0 159.4 jit_solution(8695294291010281676)
XLA Ops:
  0.6 0.7 compare_select_fusion
  1.3 0.6 reshape.12.refs_4_
  2.0 1.5 copy.10.refs_3_
  3.4 4.4 %copy.9.refs_1_ = bf16[2048,602]{1,0:T(8,128)(2,1)} copy(bf16[2048,602]{0,1:T(8,128)(2,1)} %param.7) | data formatting | bytes 4931584 | tf_op args[1]
  7.8 146.6 %shard_map.85 = (f32[1,1]{1,0:T(1,128)}, f32[602,128]{1,0:T(8,128)}, f32[128,41]{1,0:T(8,128)}) custom-call(bf16[4,2048,4096]{2,1,0:T(8,128)(2,1)} %refs_0_.1, bf16[2048,602]{1,0:T(8,128)(2,1)} %copy.9.refs_1_, f32[602,128]{1,0:T(8,128)} %refs_2_.1, f32[128,41]{1,0:T(8,128)} %copy.10.refs_3_, s32[8,256]{1,0:T(8,128)} %reshape.12.refs_4_), custom_call_target="tpu_custom_call" | custom-call | tf_op jit(solution)/shard_map/pallas_call | solution.py:457
  154.4 1.5 copy.11
  156.5 1.7 %copy.15 = f32[602,128]{1,0:T(8,128)} copy(f32[602,128]{1,0:T(8,128)} %get-tuple-element.16) | data formatting | bytes 616448

commit v2 on v1

v2 whole, which is shorter than its diff:
```python
import jax
import jax.numpy as jnp
from jax import lax
from jax.experimental import pallas as pl
from jax.experimental.pallas import tpu as pltpu
from jax.sharding import PartitionSpec as P

BF = jnp.bfloat16
F32 = jnp.float32
MESH = pl.DeviceIdType.MESH

CH = 256
NCH = 8
CP = 48
LAGS1 = (2, 4, 5)
LAGS2 = (2, 4, 6, 8)
LAGS3 = (2, 4)
L2, L3, L4 = LAGS1
M1, M2, M3, M4 = LAGS2
N1, N2 = LAGS3


def mm(a, b, ca=1, cb=0):
    return lax.dot_general(a, b, (((ca,), (cb,)), ((), ())), preferred_element_type=F32)


def kernel(
    n_class, adj, feat, w1, w2, lab, msk, loss_o, dw1_o, dw2_o,
    a_s, x_s, w2n, y1, p1, p1r, h1t, y2, zacc, zs, zr, g2, dacc, drec, g1, eacc, erec,
    cnt, cntr, f2, f2r, fr0, fs, fr1, fr2, fo, lossv,
    a_sem, x_sem, y1_ss, y1_rs, p1_ss, p1_rs, y2_ss, y2_rs, z_ss, z_rs, g2_ss, g2_rs, g1_ss, g1_rs,
    d_ss, d_rs, c_ss, c_rs, f2_ss, f2_rs, fw_ss, fw_rs,
):
    r = lax.axis_index("rep")
    i = lax.axis_index("nodes")
    nbx = r + 1 - 2 * (r % 2)
    nby = (r + 2) % 4
    r0, r1 = r % 2, r // 2
    other = 1 - i

    def near(e):
        return nbx * (1 - e) + nby * e

    def far(e):
        return nby * (1 - e) + nbx * e

    def place(a, e):
        d0 = (r0 + a % 2) % 2
        d1 = (r1 + a // 2) % 2
        return 3 * (1 - d0) * (1 - d1) + d0 * (1 - d1) * (1 + e) + (1 - d0) * d1 * (2 - e)

    def remote(src, dst, ss, rs, rep, core):
        return pltpu.make_async_remote_copy(
            src_ref=src, dst_ref=dst, send_sem=ss, recv_sem=rs, device_id=(rep, core), device_id_type=MESH
        )

    def rows_copy(chunk, slot):
        return pltpu.make_async_copy(
            adj.at[:, pl.ds(pl.multiple_of(chunk * CH, CH), CH), :], a_s.at[slot], a_sem.at[slot]
        )

    def cols_start(k, slot):
        @pl.loop(0, NCH)
        def _(g):
            for core in range(2):
                pltpu.make_async_copy(
                    adj.at[:, pl.ds(pl.multiple_of(g * CH, CH), CH), pl.ds(pl.multiple_of(core * 2048 + k * CH, CH), CH)],
                    a_s.at[slot, :, :, pl.ds(pl.multiple_of(g * 2 * CH + core * CH, CH), CH)],
                    a_sem.at[slot],
                ).start()

    x_copy = pltpu.make_async_copy(feat, x_s, x_sem)
    x_copy.start()
    rows_copy(0, 0).start()

    barrier = pltpu.get_barrier_semaphore()
    pl.semaphore_signal(barrier, inc=1, device_id=(nbx, i), device_id_type=MESH)
    pl.semaphore_signal(barrier, inc=1, device_id=(nby, i), device_id_type=MESH)
    pl.semaphore_signal(barrier, inc=1, device_id=(r, other), device_id_type=MESH)

    w2n[...] = jnp.zeros_like(w2n)
    w2n[0:n_class, :] = w2[...]
    w2t = w2n[...].astype(BF)
    total = jnp.sum(jnp.sum(msk[...].astype(F32), axis=0, keepdims=True), axis=1, keepdims=True)
    cnt[0] = jnp.broadcast_to(total, (8, 128))
    w1b = w1[...].astype(BF)
    x_copy.wait()
    for c in range(1, 4):
        rows_copy(c, c).start()

    @pl.loop(0, 4)
    def _(b):
        rows = pl.ds(pl.multiple_of(b * 512, 512), 512)
        y1[i, rows, :] = jnp.transpose(mm(w1b, x_s[:, rows], 0, 0), (1, 0)).astype(BF)

    pl.semaphore_wait(barrier, 3)

    def cnt_copy(n):
        rep = (nbx, nby, r)[n]
        core = (i, i, other)[n]
        return remote(cnt.at[n], cntr.at[n], c_ss.at[n], c_rs.at[n], rep, core)


    def y1_copy(b):
        part = y1.at[i, pl.ds(pl.multiple_of(b * 512, 512), 512), :]
        return remote(part, part, y1_ss.at[b], y1_rs.at[b], r, other)

    def y1_recv(b):
        part = y1.at[other, pl.ds(pl.multiple_of(b * 512, 512), 512), :]
        return remote(part, part, y1_ss.at[b], y1_rs.at[b], r, other)

    @pl.loop(0, 4)
    def _(b):
        y1_copy(b).start()

    cnt_copy(0).start()
    zacc[...] = jnp.zeros_like(zacc)
    dacc[...] = jnp.zeros_like(dacc)
    eacc[...] = jnp.zeros_like(eacc)
    lossv[...] = jnp.zeros_like(lossv)
    f2[0] = jnp.zeros_like(f2[0])
    cnt_copy(0).wait_recv()
    cnt[1] = cnt[0] + cntr[0]
    cnt_copy(1).start()

    @pl.loop(0, 4)
    def _(b):
        y1_recv(b).wait_recv()

    def reduce_copy(buf, rec, ss, rs, n, c, e):
        return remote(buf.at[c, n], rec.at[c, n], ss.at[n, c], rs.at[n, c], far(e) if n == 2 else near(e), i)

    def p1_copy(n, c, e):
        return reduce_copy(p1, p1r, p1_ss, p1_rs, n, c, e)

    def y2_copy(c):
        return remote(y2.at[c, i], y2.at[c, i], y2_ss.at[c], y2_rs.at[c], r, other)

    def y2_recv(c):
        return remote(y2.at[c, other], y2.at[c, other], y2_ss.at[c], y2_rs.at[c], r, other)

    def z_part(lhs, slot, g):
        rhs = a_s[slot, :, :, pl.ds(pl.multiple_of(g * 2 * CH, 2 * CH), 2 * CH)].reshape(4 * CH, 2 * CH)
        return mm(lhs, rhs, 1, 1)

    def pass2_lhs(k):
        return jnp.concatenate([y2[k, 0], y2[k, 1]], axis=1)

    def p1_slot(c):
        return c % 2 + 2 * (1 - c // 4) * ((c // 2) % 2)

    @pl.loop(0, max(NCH - 2 + L4, NCH + L3))
    def _(t):
        @pl.when(t < NCH)
        def _():
            c = t
            e = c % 2
            slot = p1_slot(c)
            rows_copy(c, slot).wait()
            res = mm(a_s[slot].reshape(4 * CH, 4096), y1[...].reshape(4096, 128))
            for a in range(4):
                p1[c, place(a, e)] = res[a * CH:(a + 1) * CH]
            p1_copy(0, c, e).start()
            p1_copy(1, c, e).start()

            @pl.when(jnp.logical_or(c < 2, c == 4))
            def _():
                rows_copy(4 + c - 2 * (c // 4), slot).start()

            @pl.when(c == 5)
            def _():
                rows_copy(7, slot).start()

            @pl.when(jnp.logical_or(c == 2, c == 3))
            def _():
                cols_start(c - 2, slot)

        @pl.when(jnp.logical_and(t >= L2, t < NCH + L2))
        def _():
            c = t - L2
            e = c % 2
            p1_copy(0, c, e).wait_recv()
            p1[c, 2] = p1[c, 2] + p1r[c, 0]
            p1_copy(2, c, e).start()

        @pl.when(jnp.logical_and(t >= L3, t < NCH + L3))
        def _():
            c = t - L3
            e = c % 2
            p1_copy(1, c, e).wait_recv()
            p1_copy(2, c, e).wait_recv()
            h = jnp.maximum(p1[c, 3] + p1r[c, 1] + p1r[c, 2], 0.0)
            ht = jnp.transpose(h, (1, 0)).astype(BF)
            h1t[c] = ht
            y2[c, i] = mm(w2t, ht).astype(BF)
            y2_copy(c).start()

        @pl.when(jnp.logical_and(t >= L4, t < NCH - 2 + L4))
        def _():
            k = t - L4
            slot = 2 + k % 2
            y2_recv(k).wait_recv()
            rows_copy(0, slot).wait()
            lhs = pass2_lhs(k)

            @pl.loop(0, 2)
            def _(gg):
                for g4 in range(4):
                    g = gg * 4 + g4
                    zacc[g] = zacc[g] + z_part(lhs, slot, g)

            cols_start(k + 2, slot)

    def z_copy(n, q, e):
        return reduce_copy(zs, zr, z_ss, z_rs, n, q, e)

    def spread_copy(buf, ss, rs, n, q, e):
        src, dst = ((3, 2), (3, 1), (2, 0))[n]
        return remote(buf.at[q, src], buf.at[q, dst], ss.at[n, q], rs.at[n, q], far(e) if n == 0 else near(e), i)

    def g2_copy(n, q, e):
        return spread_copy(g2, g2_ss, g2_rs, n, q, e)

    def g1_copy(n, q, e):
        return spread_copy(g1, g1_ss, g1_rs, n, q, e)

    cnt_copy(1).wait_recv()
    cnt[2] = cnt[1] + cntr[1]
    cnt_copy(2).start()
    for k in (NCH - 2, NCH - 1):
        y2_recv(k).wait_recv()
        rows_copy(0, 2 + k % 2).wait()
    lhs_6, lhs_7 = pass2_lhs(NCH - 2), pass2_lhs(NCH - 1)
    cnt_copy(2).wait_recv()
    count = (cnt[2] + cntr[2])[0:1, 0:1]
    class_id = lax.broadcasted_iota(jnp.int32, (CP, CH), 0)

    def gathered(buf, q, e):
        return jnp.concatenate([buf[q, place(a, e)] for a in range(4)], axis=1)

    def half(core):
        return pl.ds(pl.multiple_of(core * 2048, 2048), 2048)

    def pair_copy(src, dst, n):
        return remote(src.at[:, half(other)], dst, d_ss.at[n], d_rs.at[n], r, other)

    def p3_slot(q):
        return q % 2 + 2 * (q // 4) * (1 - (q // 2) % 2)

    def p3_chunk(q):
        return (q + 6) % NCH

    def row_of(ref, c):
        return jnp.concatenate([ref[pl.ds(2 * c, 1), :], ref[pl.ds(2 * c + 1, 1), :]], axis=1)

    @pl.loop(0, NCH + M4)
    def _(t):
        @pl.when(t < NCH)
        def _():
            q = t
            e = q % 2
            g = p3_chunk(q)
            z = zacc[g] + z_part(lhs_6, 2, g) + z_part(lhs_7, 3, g)
            for a in range(4):
                zs[q, place(a, e)] = z[:, a * CH:(a + 1) * CH]
            z_copy(0, q, e).start()
            z_copy(1, q, e).start()

            @pl.when(q == NCH - 1)
            def _():
                rows_copy(p3_chunk(4), 2).start()
                rows_copy(p3_chunk(5), 3).start()

        @pl.when(jnp.logical_and(t >= M1, t < NCH + M1))
        def _():
            q = t - M1
            e = q % 2
            z_copy(0, q, e).wait_recv()
            zs[q, 2] = zs[q, 2] + zr[q, 0]
            z_copy(2, q, e).start()

        @pl.when(jnp.logical_and(t >= M2, t < NCH + M2))
        def _():
            q = t - M2
            e = q % 2
            z_copy(1, q, e).wait_recv()
            z_copy(2, q, e).wait_recv()
            z = jnp.where(class_id < n_class, zs[q, 3] + zr[q, 1] + zr[q, 2], -1e30)
            top = jnp.max(z, axis=0, keepdims=True)
            shifted = z - top
            log_p = shifted - jnp.log(jnp.sum(jnp.exp(shifted), axis=0, keepdims=True))
            label = row_of(lab, p3_chunk(q))
            weight = row_of(msk, p3_chunk(q)).astype(F32)
            hit = class_id == label
            lossv[...] = lossv[...] - weight * jnp.sum(jnp.where(hit, log_p, 0.0), axis=0, keepdims=True)
            prob = jnp.exp(log_p)
            g2[q, 3] = ((prob - jnp.where(hit, 1.0, 0.0)) * (weight / count)).astype(BF)
            g2_copy(0, q, e).start()
            g2_copy(1, q, e).start()

        @pl.when(jnp.logical_and(t >= M3, t < NCH + M3))
        def _():
            q = t - M3
            e = q % 2
            g2_copy(0, q, e).wait_recv()
            g2_copy(2, q, e).start()

        @pl.when(t >= M4)
        def _():
            q = t - M4
            e = q % 2
            slot = p3_slot(q)
            g2_copy(1, q, e).wait_recv()
            g2_copy(2, q, e).wait_recv()

            @pl.when(q >= 2)
            def _():
                rows_copy(0, slot).wait()

            lhs = gathered(g2, q, e)
            dacc[:, half(other)] += mm(lhs, a_s[slot, :, :, half(other)].reshape(4 * CH, 2048))

            @pl.when(q == NCH - 1)
            def _():
                pair_copy(dacc, drec, 0).start()

            dacc[:, half(i)] += mm(lhs, a_s[slot, :, :, half(i)].reshape(4 * CH, 2048))

            @pl.when(q < 4)
            def _():
                rows_copy(p3_chunk(q + 2 + 2 * (q // 2)), slot).start()

    pair_copy(dacc, drec, 0).wait_recv()

    def dy2_part(c):
        cols = pl.ds(pl.multiple_of(i * 2048 + c * CH, CH), CH)
        return (dacc[:, cols] + drec[:, pl.ds(pl.multiple_of(c * CH, CH), CH)]).astype(BF)

    def p4_chunk(q):
        return p3_chunk((q + 4) % NCH)

    def f2_copy(n):
        rep = (nbx, nby, r)[n]
        core = (i, i, other)[n]
        return remote(f2.at[n], f2r.at[n], f2_ss.at[n], f2_rs.at[n], rep, core)

    @pl.loop(0, NCH + N2)
    def _(t):
        @pl.when(t < NCH)
        def _():
            q = t
            e = q % 2
            c = p4_chunk(q)
            dy2 = dy2_part(c)
            dh = mm(w2t, dy2, 0, 0)
            g1[q, 3] = jnp.where(h1t[c].astype(F32) > 0.0, dh, 0.0).astype(BF)
            g1_copy(0, q, e).start()
            g1_copy(1, q, e).start()
            f2[0, 0:CP] += mm(dy2, h1t[c], 1, 1)

        @pl.when(jnp.logical_and(t >= N1, t < NCH + N1))
        def _():
            q = t - N1
            e = q % 2
            g1_copy(0, q, e).wait_recv()
            g1_copy(2, q, e).start()

            @pl.when(q == NCH - 1)
            def _():
                f2[0, CP:CP + 8] = jnp.broadcast_to(jnp.sum(lossv[...], axis=1, keepdims=True), (8, 128))
                f2_copy(0).start()

        @pl.when(t >= N2)
        def _():
            q = t - N2
            e = q % 2
            slot = (q + 2) % 4
            g1_copy(1, q, e).wait_recv()
            g1_copy(2, q, e).wait_recv()

            @pl.when(q >= 4)
            def _():
                rows_copy(0, slot).wait()

            lhs = gathered(g1, q, e)
            eacc[:, half(other)] += mm(lhs, a_s[slot, :, :, half(other)].reshape(4 * CH, 2048))

            @pl.when(q == NCH - 1)
            def _():
                pair_copy(eacc, erec, 1).start()

            eacc[:, half(i)] += mm(lhs, a_s[slot, :, :, half(i)].reshape(4 * CH, 2048))

            @pl.when(q < 4)
            def _():
                rows_copy(p4_chunk(q + 4), slot).start()

    f2_copy(0).wait_recv()
    f2[1] = f2[0] + f2r[0]
    f2_copy(1).start()
    pair_copy(eacc, erec, 1).wait_recv()
    dy1 = (eacc[:, half(i)] + erec[...]).astype(BF)
    n_in = dw1_o.shape[0]
    dw = mm(x_s[...], dy1, 1, 1)
    fs[0, 0] = dw[0:320]
    fs[0, 1, n_in - 320 - 2:320] = jnp.zeros((642 - n_in, 128), F32)
    fs[0, 1, 0:n_in - 320] = dw[320:n_in]

    def pair_half():
        return remote(fs.at[0, other], fr0, fw_ss.at[0], fw_rs.at[0], r, other)

    def quarter(n, h):
        rep = nbx * (1 - (n + h) % 2) + nby * ((n + h) % 2)
        return remote(
            fs.at[1 + n, 0, pl.ds(h * 160, 160)], fr1.at[n, pl.ds(h * 160, 160)],
            fw_ss.at[1 + 2 * n + h], fw_rs.at[1 + 2 * n + h], rep, i,
        )

    def back():
        return remote(fs.at[2, 1], fr2, fw_ss.at[5], fw_rs.at[5], r, other)

    pair_half().start()
    pair_half().wait_recv()
    fs[1, 0] = fs[0, i] + fr0[...]
    for h in range(2):
        quarter(0, h).start()
    for h in range(2):
        quarter(0, h).wait_recv()
        fs[2, 0, h * 160:(h + 1) * 160] = fs[1, 0, h * 160:(h + 1) * 160] + fr1[0, h * 160:(h + 1) * 160]
        quarter(1, h).start()
    f2_copy(1).wait_recv()
    f2[2] = f2[1] + f2r[1]
    f2_copy(2).start()
    for h in range(2):
        quarter(1, h).wait_recv()
    fs[2, 1] = fs[2, 0] + fr1[1]
    back().start()
    f2_copy(2).wait_recv()
    f_sum = f2[2] + f2r[2]
    dw2_o[...] = f_sum[0:n_class]
    loss_o[...] = f_sum[CP:CP + 1, 0:1] / count
    back().wait_recv()
    fo[i] = fs[2, 1]
    fo[other] = fr2[...]
    dw1_o[0:320] = fo[0]
    dw1_o[320:n_in] = fo[1, 0:n_in - 320]

    @pl.loop(0, 4)
    def _(b):
        y1_copy(b).wait_send()

    @pl.loop(0, NCH)
    def _(c):
        e = c % 2
        y2_copy(c).wait_send()
        for n in range(3):
            p1_copy(n, c, e).wait_send()
            z_copy(n, c, e).wait_send()
            g2_copy(n, c, e).wait_send()
            g1_copy(n, c, e).wait_send()

    for n in range(3):
        cnt_copy(n).wait_send()
        f2_copy(n).wait_send()
    pair_copy(dacc, drec, 0).wait_send()
    pair_copy(eacc, erec, 1).wait_send()
    pair_half().wait_send()
    for n in range(2):
        for h in range(2):
            quarter(n, h).wait_send()
    back().wait_send()


def emit(*refs):
    for src, dst in zip(refs[:3], refs[3:]):
        dst[...] = src[...]


def solution(mesh):
    def device_step(adj, feat, w1, w2, labels, mask):
        n_in, n_hid = w1.shape
        n_class = w2.shape[1]
        vmem = pl.BlockSpec(memory_space=pltpu.VMEM)
        hbm = pl.BlockSpec(memory_space=pl.ANY)
        dma = pltpu.SemaphoreType.DMA

        def body(*refs):
            kernel(n_class, *refs)

        sums = pl.pallas_call(
            body,
            out_shape=(
                jax.ShapeDtypeStruct((1, 1), F32),
                jax.ShapeDtypeStruct((n_in, n_hid), F32),
                jax.ShapeDtypeStruct((n_class, n_hid), F32),
            ),
            in_specs=[hbm, hbm, vmem, vmem, vmem, vmem],
            out_specs=(vmem, vmem, vmem),
            scratch_shapes=[
                pltpu.VMEM((4, 4, CH, 4096), BF),
                pltpu.VMEM((n_in, 2048), BF),
                pltpu.VMEM((CP, 128), F32),
                pltpu.VMEM((2, 2048, 128), BF),
                pltpu.VMEM((NCH, 4, CH, 128), F32),
                pltpu.VMEM((NCH, 3, CH, 128), F32),
                pltpu.VMEM((NCH, 128, CH), BF),
                pltpu.VMEM((NCH, 2, CP, CH), BF),
                pltpu.VMEM((NCH, CP, 4 * CH), F32),
                pltpu.VMEM((NCH, 4, CP, CH), F32),
                pltpu.VMEM((NCH, 3, CP, CH), F32),
                pltpu.VMEM((NCH, 4, CP, CH), BF),
                pltpu.VMEM((CP, 4096), F32),
                pltpu.VMEM((CP, 2048), F32),
                pltpu.VMEM((NCH, 4, 128, CH), BF),
                pltpu.VMEM((128, 4096), F32),
                pltpu.VMEM((128, 2048), F32),
                pltpu.VMEM((3, 8, 128), F32),
                pltpu.VMEM((3, 8, 128), F32),
                pltpu.VMEM((3, CP + 8, 128), F32),
                pltpu.VMEM((3, CP + 8, 128), F32),
                pltpu.VMEM((320, 128), F32),
                pltpu.VMEM((3, 2, 320, 128), F32),
                pltpu.VMEM((2, 320, 128), F32),
                pltpu.VMEM((320, 128), F32),
                pltpu.VMEM((2, 320, 128), F32),
                pltpu.VMEM((1, CH), F32),
                dma((4,)), dma(()),
                dma((4,)), dma((4,)),
                dma((3, NCH)), dma((3, NCH)),
                dma((NCH,)), dma((NCH,)),
                dma((3, NCH)), dma((3, NCH)),
                dma((3, NCH)), dma((3, NCH)),
                dma((3, NCH)), dma((3, NCH)),
                dma((2,)), dma((2,)),
                dma((3,)), dma((3,)),
                dma((3,)), dma((3,)),
                dma((6,)), dma((6,)),
            ],
            compiler_params=pltpu.CompilerParams(
                collective_id=0, has_side_effects=True, vmem_limit_bytes=67043328
            ),
        )(adj, feat.T, w1, w2.T, labels.reshape(16, 128), mask.reshape(16, 128))
        loss, dw1, dw2 = pl.pallas_call(
            emit,
            out_shape=tuple(jax.ShapeDtypeStruct(x.shape, x.dtype) for x in sums),
            in_specs=[vmem] * 3,
            out_specs=(vmem, vmem, vmem),
        )(*sums)
        return loss.reshape(()), dw1, dw2.T

    row_spec = P(("rep", "nodes"))
    return jax.shard_map(
        device_step,
        mesh=mesh,
        in_specs=(P(None, "nodes", "rep"), row_spec, P(), P(), row_spec, row_spec),
        out_specs=(P(), P(), P()),
        check_vma=False,
    )
```

time: 160 us -> 130 us (0.81)
  Pallas kernels: 147 us -> 129 us
  local copies, waits for them, and re-layouts: 9.67 us -> 0 us
  between operations: 2.4 us -> 0.64 us
    pallas_call x1, Pallas kernels: 147 us -> 126 us  [device_step(): pl.pallas_call(body, out_shape=(jax.ShapeDtypeStruct((1, 1), F32), jax.Sh...]
    unnamed x4 -> x0, local copies, waits for them, and re-layouts: 9.07 us -> none
    pallas_call x0 -> x1, Pallas kernels: none -> 2.34 us  [device_step(): pl.pallas_call(emit, out_shape=tuple((jax.ShapeDtypeStruct(x.shape, x.dty...]
where the time goes in v2:
time: 130 us; the launch traced here: 129 us
  Pallas kernels  129 us (99%)
    pallas_call x1, Pallas kernels, device_step(): pl.pallas_call(body, out_shape=(jax.ShapeDtypeStruct((1, 1), F32), jax.Sh...  126 us

profile of v2, /device:TPU:0, one launch (start us, length us, event | category | flops | bytes accessed | tf_op | source)
XLA Modules:
  0.0 129.4 jit_solution(6902951376356633918)
XLA Ops:
  0.6 126.4 %shard_map.85 = (f32[1,1]{1,0:T(1,128)}, f32[602,128]{1,0:T(8,128)}, f32[41,128]{1,0:T(8,128)}) custom-call(bf16[4,2048,4096]{2,1,0:T(8,128)(2,1)} %refs_0_.1, bf16[602,2048]{1,0:T(8,128)(2,1)} %bitcast.6, f32[602,128]{1,0:T(8,128)} %refs_2_.1, f32[41,128]{1,0:T(8,128)} %bitcast.7, s32[16,128]{1,0:T(8,128)} %bitcast.8, s32[16,128]{1,0:T(8,128)} %bitcast.9), custom_call_target="tpu_custom_call" | custom-call | tf_op jit(solution)/shard_map/pallas_call | solution.py:490
  127.0 2.3 %shard_map.86 = (f32[1,1]{1,0:T(1,128)}, f32[602,128]{1,0:T(8,128)}, f32[41,128]{1,0:T(8,128)}) custom-call(f32[1,1]{1,0:T(1,128)} %get-tuple-element.9.refs_0_, f32[602,128]{1,0:T(8,128)} %get-tuple-element.10.refs_1_, f32[41,128]{1,0:T(8,128)} %get-tuple-element.11.refs_2_), custom_call_target="tpu_custom_call" | custom-call | tf_op jit(solution)/shard_map/pallas_call | solution.py:543

commit v3 on v2

v3 whole, which is shorter than its diff:
```python
import jax
import jax.numpy as jnp
from jax import lax
from jax.experimental import pallas as pl
from jax.experimental.pallas import tpu as pltpu
from jax.sharding import PartitionSpec as P

BF = jnp.bfloat16
F32 = jnp.float32
MESH = pl.DeviceIdType.MESH

CH = 256
NCH = 8
CP = 48
HID = 128
ND = 2048
NCOL = 2 * ND
HR = 304
QR = HR // 2
LAGS1 = (2, 4, 5)
LAGS2 = (2, 4, 6, 8)
LAGS3 = (0, 1, 3)
L2, L3, L4 = LAGS1
M1, M2, M3, M4 = LAGS2
N1, N2, N3 = LAGS3
LN = 1
LZ = 1
LG = 1
LB = 1
NROW = 4


def mm(a, b, ca=1, cb=0):
    return lax.dot_general(a, b, (((ca,), (cb,)), ((), ())), preferred_element_type=F32)


def kernel(
    n_class, adj, feat, w1, w2, lab, msk, loss_o, dw1_o, dw2_o,
    a_s, x_s, w2n, y1, p1, p1r, h1t, y2, zacc, zs, zr, g2, dacc, drec, g1, eacc, erec,
    cnt, cntr, f2, f2r, fr0, fs, fr1, lossv,
    a_sem, piece_sem, x_sem, y1_ss, y1_rs, p1_ss, p1_rs, y2_ss, y2_rs, z_ss, z_rs, g2_ss, g2_rs, g1_ss, g1_rs,
    dp_ss, dp_rs, d_ss, d_rs, c_ss, c_rs, f2_ss, f2_rs, fw_ss, fw_rs,
):
    r = lax.axis_index("rep")
    i = lax.axis_index("nodes")
    nbx = r + 1 - 2 * (r % 2)
    nby = (r + 2) % 4
    r0, r1 = r % 2, r // 2
    other = 1 - i

    def near(e):
        return nbx * (1 - e) + nby * e

    def far(e):
        return nby * (1 - e) + nbx * e

    def place(a, e):
        d0 = (r0 + a % 2) % 2
        d1 = (r1 + a // 2) % 2
        return 3 * (1 - d0) * (1 - d1) + d0 * (1 - d1) * (1 + e) + (1 - d0) * d1 * (2 - e)

    def remote(src, dst, ss, rs, rep, core):
        return pltpu.make_async_remote_copy(
            src_ref=src, dst_ref=dst, send_sem=ss, recv_sem=rs, device_id=(rep, core), device_id_type=MESH
        )

    def rows_copy(chunk, slot):
        return pltpu.make_async_copy(
            adj.at[:, pl.ds(pl.multiple_of(chunk * CH, CH), CH), :], a_s.at[slot], a_sem.at[slot]
        )

    def cols_start(k, slot, sem_of):
        @pl.loop(0, NCH)
        def _(n):
            g = (n + 6) % NCH
            for core in range(2):
                pltpu.make_async_copy(
                    adj.at[:, pl.ds(pl.multiple_of(g * CH, CH), CH), pl.ds(pl.multiple_of(core * ND + k * CH, CH), CH)],
                    a_s.at[slot, :, :, pl.ds(pl.multiple_of(g * 2 * CH + core * CH, CH), CH)],
                    sem_of(g),
                ).start()

    def cols_piece_wait(slot, g):
        pltpu.make_async_copy(
            adj.at[:, pl.ds(0, CH), pl.ds(0, 2 * CH)],
            a_s.at[slot, :, :, pl.ds(pl.multiple_of(g * 2 * CH, 2 * CH), 2 * CH)],
            piece_sem.at[slot - 2, g],
        ).wait()

    x_copy = pltpu.make_async_copy(feat, x_s, x_sem)
    x_copy.start()
    rows_copy(0, 0).start()

    barrier = pltpu.get_barrier_semaphore()
    pl.semaphore_signal(barrier, inc=1, device_id=(nbx, i), device_id_type=MESH)
    pl.semaphore_signal(barrier, inc=1, device_id=(nby, i), device_id_type=MESH)
    pl.semaphore_signal(barrier, inc=1, device_id=(r, other), device_id_type=MESH)

    w2n[...] = jnp.zeros_like(w2n)
    w2n[0:n_class, :] = w2[...]
    w2t = w2n[...].astype(BF)
    total = jnp.sum(jnp.sum(msk[...].astype(F32), axis=0, keepdims=True), axis=1, keepdims=True)
    cnt[0] = jnp.broadcast_to(total, (8, HID))
    w1b = w1[...].astype(BF)
    x_copy.wait()
    for c in range(1, 4):
        rows_copy(c, c).start()

    @pl.loop(0, 4)
    def _(b):
        rows = pl.ds(pl.multiple_of(b * 512, 512), 512)
        y1[i, rows, :] = jnp.transpose(mm(w1b, x_s[:, rows], 0, 0), (1, 0)).astype(BF)

    pl.semaphore_wait(barrier, 3)

    def cnt_copy(n):
        rep = (nbx, nby, r)[n]
        core = (i, i, other)[n]
        return remote(cnt.at[n], cntr.at[n], c_ss.at[n], c_rs.at[n], rep, core)


    def y1_copy(b):
        part = y1.at[i, pl.ds(pl.multiple_of(b * 512, 512), 512), :]
        return remote(part, part, y1_ss.at[b], y1_rs.at[b], r, other)

    def y1_recv(b):
        part = y1.at[other, pl.ds(pl.multiple_of(b * 512, 512), 512), :]
        return remote(part, part, y1_ss.at[b], y1_rs.at[b], r, other)

    @pl.loop(0, 4)
    def _(b):
        y1_copy(b).start()

    cnt_copy(0).start()
    zacc[...] = jnp.zeros_like(zacc)
    dacc[...] = jnp.zeros_like(dacc)
    eacc[...] = jnp.zeros_like(eacc)
    lossv[...] = jnp.zeros_like(lossv)
    f2[0] = jnp.zeros_like(f2[0])
    @pl.loop(0, 4)
    def _(b):
        y1_recv(b).wait_recv()

    def reduce_copy(buf, rec, ss, rs, n, c, e):
        return remote(buf.at[c, n], rec.at[c, n], ss.at[n, c], rs.at[n, c], far(e) if n == 2 else near(e), i)

    def p1_copy(n, c, e):
        return reduce_copy(p1, p1r, p1_ss, p1_rs, n, c, e)

    def y2_copy(c):
        return remote(y2.at[c, i], y2.at[c, i], y2_ss.at[c], y2_rs.at[c], r, other)

    def y2_recv(c):
        return remote(y2.at[c, other], y2.at[c, other], y2_ss.at[c], y2_rs.at[c], r, other)

    def z_part(lhs, slot, g):
        rhs = a_s[slot, :, :, pl.ds(pl.multiple_of(g * 2 * CH, 2 * CH), 2 * CH)].reshape(4 * CH, 2 * CH)
        return mm(lhs, rhs, 1, 1)

    def pass2_lhs(k):
        return jnp.concatenate([y2[k, 0], y2[k, 1]], axis=1)

    def p1_slot(c):
        return c % 2 + 2 * (1 - c // 4) * ((c // 2) % 2)

    @pl.loop(0, max(NCH - 2 + L4, NCH + L3))
    def _(t):
        @pl.when(t < NCH)
        def _():
            c = t
            e = c % 2
            slot = p1_slot(c)
            rows_copy(c, slot).wait()
            res = mm(a_s[slot].reshape(4 * CH, NCOL), y1[...].reshape(NCOL, HID))
            for a in range(4):
                p1[c, place(a, e)] = res[a * CH:(a + 1) * CH]
            p1_copy(0, c, e).start()
            if LB == 0:
                p1_copy(1, c, e).start()

            @pl.when(jnp.logical_or(c < 2, c == 4))
            def _():
                rows_copy(4 + c - 2 * (c // 4), slot).start()

            @pl.when(c == 5)
            def _():
                rows_copy(7, slot).start()

            @pl.when(jnp.logical_or(c == 2, c == 3))
            def _():
                cols_start(c - 2, slot, lambda g: a_sem.at[slot])

        @pl.when(jnp.logical_and(t >= L2, t < NCH + L2))
        def _():
            c = t - L2
            e = c % 2
            p1_copy(0, c, e).wait_recv()
            p1[c, 2] = p1[c, 2] + p1r[c, 0]
            p1_copy(2, c, e).start()

        if LB:
            @pl.when(jnp.logical_and(t >= LB, t < NCH + LB))
            def _():
                p1_copy(1, t - LB, (t - LB) % 2).start()

        for n in range(2):
            @pl.when(t == 3 + 6 * n)
            def _():
                cnt_copy(n).wait_recv()
                cnt[n + 1] = cnt[n] + cntr[n]
                cnt_copy(n + 1).start()

        @pl.when(jnp.logical_and(t >= L3, t < NCH + L3))
        def _():
            c = t - L3
            e = c % 2
            p1_copy(1, c, e).wait_recv()
            p1_copy(2, c, e).wait_recv()
            h = jnp.maximum(p1[c, 3] + p1r[c, 1] + p1r[c, 2], 0.0)
            ht = jnp.transpose(h, (1, 0)).astype(BF)
            h1t[c] = ht
            y2[c, i] = mm(w2t, ht).astype(BF)
            y2_copy(c).start()

        @pl.when(jnp.logical_and(t >= L4, t < NCH - 2 + L4))
        def _():
            k = t - L4
            slot = 2 + k % 2
            y2_recv(k).wait_recv()
            rows_copy(0, slot).wait()
            lhs = pass2_lhs(k)

            for g in range(NCH):
                zacc[g] = zacc[g] + z_part(lhs, slot, g)

            @pl.when(k < NCH - 4)
            def _():
                cols_start(k + 2, slot, lambda g: a_sem.at[slot])

            @pl.when(k >= NCH - 4)
            def _():
                cols_start(k + 2, slot, lambda g: piece_sem.at[slot - 2, g])

    def z_copy(n, q, e):
        return reduce_copy(zs, zr, z_ss, z_rs, n, q, e)

    def spread_copy(buf, ss, rs, n, q, e):
        src, dst = ((3, 2), (3, 1), (2, 0))[n]
        return remote(buf.at[q, src], buf.at[q, dst], ss.at[n, q], rs.at[n, q], far(e) if n == 0 else near(e), i)

    def g2_copy(n, q, e):
        return spread_copy(g2, g2_ss, g2_rs, n, q, e)

    def g1_copy(n, q, e):
        return spread_copy(g1, g1_ss, g1_rs, n, q, e)

    for k in (NCH - 2, NCH - 1):
        y2_recv(k).wait_recv()
    lhs_6, lhs_7 = pass2_lhs(NCH - 2), pass2_lhs(NCH - 1)
    cnt_copy(2).wait_recv()
    count = (cnt[2] + cntr[2])[0:1, 0:1]
    class_id = lax.broadcasted_iota(jnp.int32, (CP, CH), 0)

    def gathered(buf, q, e):
        return jnp.concatenate([buf[q, place(a, e)] for a in range(4)], axis=1)

    def half(core):
        return pl.ds(pl.multiple_of(core * ND, ND), ND)

    def pair_copy():
        return remote(eacc.at[:, half(other)], erec, d_ss, d_rs, r, other)

    def p3_slot(q):
        return q % 2 + 2 * (q // 4) * (1 - (q // 2) % 2)

    def p3_chunk(q):
        return (q + 6) % NCH

    def row_of(ref, c):
        return jnp.concatenate([ref[pl.ds(2 * c, 1), :], ref[pl.ds(2 * c + 1, 1), :]], axis=1)

    @pl.loop(0, max(NCH + M3, NROW + M4))
    def _(t):
        @pl.when(t < NCH)
        def _():
            q = t
            e = q % 2
            g = p3_chunk(q)
            cols_piece_wait(2, g)
            cols_piece_wait(3, g)
            z = zacc[g] + z_part(lhs_6, 2, g) + z_part(lhs_7, 3, g)
            for a in range(4):
                zs[q, place(a, e)] = z[:, a * CH:(a + 1) * CH]
            z_copy(0, q, e).start()

            @pl.when(q == NCH - 1)
            def _():
                rows_copy(p3_chunk(4), 2).start()
                rows_copy(p3_chunk(5), 3).start()

        @pl.when(jnp.logical_and(t >= M1, t < NCH + M1))
        def _():
            q = t - M1
            e = q % 2
            z_copy(0, q, e).wait_recv()
            zs[q, 2] = zs[q, 2] + zr[q, 0]
            z_copy(2, q, e).start()

        @pl.when(jnp.logical_and(t >= LZ, t < NCH + LZ))
        def _():
            z_copy(1, t - LZ, (t - LZ) % 2).start()

        @pl.when(jnp.logical_and(t >= M2, t < NCH + M2))
        def _():
            q = t - M2
            e = q % 2
            z_copy(1, q, e).wait_recv()
            z_copy(2, q, e).wait_recv()
            z = jnp.where(class_id < n_class, zs[q, 3] + zr[q, 1] + zr[q, 2], -1e30)
            top = jnp.max(z, axis=0, keepdims=True)
            shifted = z - top
            log_p = shifted - jnp.log(jnp.sum(jnp.exp(shifted), axis=0, keepdims=True))
            label = row_of(lab, p3_chunk(q))
            weight = row_of(msk, p3_chunk(q)).astype(F32)
            hit = class_id == label
            lossv[...] = lossv[...] - weight * jnp.sum(jnp.where(hit, log_p, 0.0), axis=0, keepdims=True)
            prob = jnp.exp(log_p)
            g2[q, 3] = ((prob - jnp.where(hit, 1.0, 0.0)) * (weight / count)).astype(BF)
            g2_copy(0, q, e).start()

        @pl.when(jnp.logical_and(t >= M3, t < NCH + M3))
        def _():
            q = t - M3
            e = q % 2
            g2_copy(0, q, e).wait_recv()
            g2_copy(2, q, e).start()

        @pl.when(jnp.logical_and(t >= M2 + LG, t < NCH + M2 + LG))
        def _():
            g2_copy(1, t - M2 - LG, (t - M2 - LG) % 2).start()

        @pl.when(jnp.logical_and(t >= M4, t < NROW + M4))
        def _():
            q = t - M4
            e = q % 2
            slot = p3_slot(q)
            g2_copy(1, q, e).wait_recv()
            g2_copy(2, q, e).wait_recv()

            @pl.when(q >= 2)
            def _():
                rows_copy(0, slot).wait()

            lhs = gathered(g2, q, e)
            dacc[...] += mm(lhs, a_s[slot].reshape(4 * CH, NCOL))

            @pl.when(q < 4)
            def _():
                rows_copy(p3_chunk(q + 2 + 2 * (q // 2)), slot).start()

    for q in range(NROW, NCH):
        g2_copy(1, q, q % 2).wait_recv()
        g2_copy(2, q, q % 2).wait_recv()
        rows_copy(0, p3_slot(q)).wait()

    PW = 2 * CH

    def cols_of(core, pair):
        return pl.ds(pl.multiple_of(core * ND + pair * PW, PW), PW)

    def dacc_copy(pair):
        return remote(dacc.at[:, cols_of(other, pair)], drec.at[pair], dp_ss.at[pair], dp_rs.at[pair], r, other)

    def finish_pass3(core, pair):
        cols = cols_of(core, pair)
        acc = dacc[:, cols]
        for q in range(NROW, NCH):
            acc = acc + mm(gathered(g2, q, q % 2), a_s[p3_slot(q), :, :, cols].reshape(4 * CH, PW))
        dacc[:, cols] = acc

    def p4_chunk(q):
        return p3_chunk((q + 4) % NCH)

    def f2_copy(n):
        rep = (nbx, nby, r)[n]
        core = (i, i, other)[n]
        return remote(f2.at[n], f2r.at[n], f2_ss.at[n], f2_rs.at[n], rep, core)

    NP = NCH // 2

    @pl.loop(0, NP + N3)
    def _(t):
        @pl.when(t < NP)
        def _():
            pair = (t + 1) % NP
            finish_pass3(other, pair)
            dacc_copy(pair).start()
            finish_pass3(i, pair)

        @pl.when(jnp.logical_and(t >= N1, t < NP + N1))
        def _():
            pair = (t - N1 + 1) % NP
            dacc_copy(pair).wait_recv()
            dy2 = (dacc[:, cols_of(i, pair)] + drec[pair]).astype(BF)
            dh = mm(w2t, dy2, 0, 0)
            for e in range(2):
                q = 2 * (t - N1) + e
                part = dh[:, e * CH:(e + 1) * CH]
                g1[q, 3] = jnp.where(h1t[2 * pair + e].astype(F32) > 0.0, part, 0.0).astype(BF)
                g1_copy(0, q, e).start()
            for e in range(2):
                f2[0, 0:CP] += mm(dy2[:, e * CH:(e + 1) * CH], h1t[2 * pair + e], 1, 1)

            @pl.when(t == NP - 1 + N1)
            def _():
                f2[0, CP:CP + 8] = jnp.broadcast_to(jnp.sum(lossv[...], axis=1, keepdims=True), (8, HID))
                f2_copy(0).start()

        @pl.when(jnp.logical_and(t >= LN, t < NP + LN))
        def _():
            for e in range(2):
                g1_copy(1, 2 * (t - LN) + e, e).start()

        @pl.when(jnp.logical_and(t >= N2, t < NP + N2))
        def _():
            for e in range(2):
                q = 2 * (t - N2) + e
                g1_copy(0, q, e).wait_recv()
                g1_copy(2, q, e).start()

        @pl.when(t >= N3)
        def _():
            for e in range(2):
                q = 2 * (t - N3) + e
                slot = (q + 2) % 4
                g1_copy(1, q, e).wait_recv()
                g1_copy(2, q, e).wait_recv()

                @pl.when(q >= 4)
                def _():
                    rows_copy(0, slot).wait()

                lhs = gathered(g1, q, e)

                @pl.when(q < NCH - 1)
                def _():
                    eacc[...] += mm(lhs, a_s[slot].reshape(4 * CH, NCOL))

                if e == 1:

                    @pl.when(q == NCH - 1)
                    def _():
                        for core in (other, i):
                            cols = half(core)
                            eacc[:, cols] += mm(lhs, a_s[slot, :, :, cols].reshape(4 * CH, ND))
                            if core is other:
                                pair_copy().start()

                @pl.when(q < 4)
                def _():
                    rows_copy(p4_chunk(q + 4), slot).start()

    f2_copy(0).wait_recv()
    f2[1] = f2[0] + f2r[0]
    f2_copy(1).start()
    pair_copy().wait_recv()
    dy1 = (eacc[:, half(i)] + erec[...]).astype(BF)
    n_in = w1.shape[0]
    dw = mm(x_s[...], dy1, 1, 1)
    fs[0, 0] = dw[:HR]
    fs[0, 1, HR - 8:] = jnp.zeros((8, HID), F32)
    fs[0, 1, :n_in - HR] = dw[HR:]

    def pair_half():
        return remote(fs.at[0, other], fr0, fw_ss.at[0], fw_rs.at[0], r, other)

    def quarter(n, h):
        rep = nbx * (1 - (n + h) % 2) + nby * ((n + h) % 2)
        return remote(
            fs.at[1 + n, 0, pl.ds(h * QR, QR)], fr1.at[n, pl.ds(h * QR, QR)],
            fw_ss.at[1 + 2 * n + h], fw_rs.at[1 + 2 * n + h], rep, i,
        )

    def back():
        return remote(fs.at[2, 1], dw1_o.at[i], fw_ss.at[5], fw_rs.at[5], r, other)

    def back_recv():
        return remote(fs.at[2, 1], dw1_o.at[other], fw_ss.at[5], fw_rs.at[5], r, other)

    pair_half().start()
    pair_half().wait_recv()
    fs[1, 0] = fs[0, i] + fr0[...]
    for h in range(2):
        quarter(0, h).start()
    for h in range(2):
        quarter(0, h).wait_recv()
        rows = pl.ds(h * QR, QR)
        fs[2, 0, rows] = fs[1, 0, rows] + fr1[0, rows]
        quarter(1, h).start()
    f2_copy(1).wait_recv()
    f2[2] = f2[1] + f2r[1]
    f2_copy(2).start()
    for h in range(2):
        quarter(1, h).wait_recv()
    fs[2, 1] = fs[2, 0] + fr1[1]
    back().start()
    keep = pltpu.make_async_copy(fs.at[2, 1], dw1_o.at[i], x_sem)
    keep.start()
    f2_copy(2).wait_recv()
    f_sum = f2[2] + f2r[2]
    dw2_o[...] = f_sum[0:n_class]
    loss_o[...] = f_sum[CP:CP + 1, 0:1] / count
    keep.wait()
    back_recv().wait_recv()

    @pl.loop(0, 4)
    def _(b):
        y1_copy(b).wait_send()

    @pl.loop(0, NCH)
    def _(c):
        e = c % 2
        y2_copy(c).wait_send()
        for n in range(3):
            p1_copy(n, c, e).wait_send()
            z_copy(n, c, e).wait_send()
            g2_copy(n, c, e).wait_send()
            g1_copy(n, c, e).wait_send()

    for pair in range(NCH // 2):
        dacc_copy(pair).wait_send()
    for n in range(3):
        cnt_copy(n).wait_send()
        f2_copy(n).wait_send()
    pair_copy().wait_send()
    pair_half().wait_send()
    for n in range(2):
        for h in range(2):
            quarter(n, h).wait_send()
    back().wait_send()


def emit(loss, dw1, dw2, loss_o, dw1_o, dw2_o):
    loss_o[...] = loss[...]
    dw2_o[...] = dw2[...]
    dw1_o[:HR] = dw1[0]
    dw1_o[HR:] = dw1[1, :dw1_o.shape[0] - HR]


def solution(mesh):
    def device_step(adj, feat, w1, w2, labels, mask):
        n_in, n_hid = w1.shape
        n_class = w2.shape[1]
        vmem = pl.BlockSpec(memory_space=pltpu.VMEM)
        hbm = pl.BlockSpec(memory_space=pl.ANY)
        dma = pltpu.SemaphoreType.DMA
        per = (3, NCH)

        def body(*refs):
            kernel(n_class, *refs)

        sums = pl.pallas_call(
            body,
            out_shape=(
                jax.ShapeDtypeStruct((1, 1), F32),
                jax.ShapeDtypeStruct((2, HR, n_hid), F32),
                jax.ShapeDtypeStruct((n_class, n_hid), F32),
            ),
            in_specs=[hbm, hbm, vmem, vmem, vmem, vmem],
            out_specs=(vmem, hbm, vmem),
            scratch_shapes=[
                pltpu.VMEM((4, 4, CH, NCOL), BF),
                pltpu.VMEM((n_in, ND), BF),
                pltpu.VMEM((CP, HID), F32),
                pltpu.VMEM((2, ND, HID), BF),
                pltpu.VMEM((NCH, 4, CH, HID), F32),
                pltpu.VMEM((NCH, 3, CH, HID), F32),
                pltpu.VMEM((NCH, HID, CH), BF),
                pltpu.VMEM((NCH, 2, CP, CH), BF),
                pltpu.VMEM((NCH, CP, 4 * CH), F32),
                pltpu.VMEM((NCH, 4, CP, CH), F32),
                pltpu.VMEM((NCH, 3, CP, CH), F32),
                pltpu.VMEM((NCH, 4, CP, CH), BF),
                pltpu.VMEM((CP, NCOL), F32),
                pltpu.VMEM((NCH // 2, CP, 2 * CH), F32),
                pltpu.VMEM((NCH, 4, HID, CH), BF),
                pltpu.VMEM((HID, NCOL), F32),
                pltpu.VMEM((HID, ND), F32),
                pltpu.VMEM((3, 8, HID), F32),
                pltpu.VMEM((3, 8, HID), F32),
                pltpu.VMEM((3, CP + 8, HID), F32),
                pltpu.VMEM((3, CP + 8, HID), F32),
                pltpu.VMEM((HR, HID), F32),
                pltpu.VMEM((3, 2, HR, HID), F32),
                pltpu.VMEM((2, HR, HID), F32),
                pltpu.VMEM((1, CH), F32),
                dma((4,)), dma((2, NCH)), dma(()),
                *[
                    dma(n) for n in ((4,), per, (NCH,), per, per, per, (NCH // 2,), (), (3,), (3,), (6,))
                    for _ in ("send", "receive")
                ],
            ],
            compiler_params=pltpu.CompilerParams(
                collective_id=0, has_side_effects=True, vmem_limit_bytes=67043328
            ),
        )(adj, feat.T, w1, w2.T, labels.reshape(-1, HID), mask.reshape(-1, HID))
        loss, dw1, dw2 = pl.pallas_call(
            emit,
            out_shape=(
                jax.ShapeDtypeStruct((1, 1), F32),
                jax.ShapeDtypeStruct((n_in, n_hid), F32),
                jax.ShapeDtypeStruct((n_class, n_hid), F32),
            ),
            in_specs=[vmem] * 3,
            out_specs=(vmem, vmem, vmem),
        )(*sums)
        return loss.reshape(()), dw1, dw2.T

    row_spec = P(("rep", "nodes"))
    return jax.shard_map(
        device_step,
        mesh=mesh,
        in_specs=(P(None, "nodes", "rep"), row_spec, P(), P(), row_spec, row_spec),
        out_specs=(P(), P(), P()),
        check_vma=False,
    )
```

time: 130 us -> 124 us (0.954)
  Pallas kernels: 129 us -> 123 us
    pallas_call x1, Pallas kernels: 126 us -> 121 us  [device_step(): pl.pallas_call(body, out_shape=(jax.ShapeDtypeStruct((1, 1), F32), jax.Sh...]
where the time goes in v3:
time: 124 us
  Pallas kernels  123 us (99%)
    pallas_call x1, Pallas kernels, device_step(): pl.pallas_call(body, out_shape=(jax.ShapeDtypeStruct((1, 1), F32), jax.Sh...  121 us

profile of v3, /device:TPU:0, one launch (start us, length us, event | category | flops | bytes accessed | tf_op | source)
XLA Modules:
  0.0 124.0 jit_solution(9429234962917202593)
XLA Ops:
  0.6 121.0 %shard_map.85 = (f32[1,1]{1,0:T(1,128)}, f32[2,304,128]{2,1,0:T(8,128)}, f32[41,128]{1,0:T(8,128)}) custom-call(bf16[4,2048,4096]{2,1,0:T(8,128)(2,1)} %refs_0_.1, bf16[602,2048]{1,0:T(8,128)(2,1)} %bitcast.6, f32[602,128]{1,0:T(8,128)} %refs_2_.1, f32[41,128]{1,0:T(8,128)} %bitcast.7, s32[16,128]{1,0:T(8,128)} %bitcast.8, s32[16,128]{1,0:T(8,128)} %bitcast.9), custom_call_target="tpu_custom_call" | custom-call | tf_op jit(solution)/shard_map/pallas_call | solution.py:562
  121.6 2.3 %shard_map.86 = (f32[1,1]{1,0:T(1,128)}, f32[602,128]{1,0:T(8,128)}, f32[41,128]{1,0:T(8,128)}) custom-call(f32[1,1]{1,0:T(1,128)} %get-tuple-element.9.loss, f32[2,304,128]{2,1,0:T(8,128)} %get-tuple-element.10.dw1, f32[41,128]{1,0:T(8,128)} %get-tuple-element.11.dw2), custom_call_target="tpu_custom_call" | custom-call | tf_op jit(solution)/shard_map/pallas_call | solution.py:607

commit v4 on v3

--- a/solution.py
+++ b/solution.py
@@ -35,10 +35,10 @@
 
 
 def kernel(
-    n_class, adj, feat, w1, w2, lab, msk, loss_o, dw1_o, dw2_o,
+    n_class, adj, feat, w1_h, w2_h, lab_h, msk_h, dw1_o, rest_o, w1, w2, lab, msk, rest,
     a_s, x_s, w2n, y1, p1, p1r, h1t, y2, zacc, zs, zr, g2, dacc, drec, g1, eacc, erec,
     cnt, cntr, f2, f2r, fr0, fs, fr1, lossv,
-    a_sem, piece_sem, x_sem, y1_ss, y1_rs, p1_ss, p1_rs, y2_ss, y2_rs, z_ss, z_rs, g2_ss, g2_rs, g1_ss, g1_rs,
+    a_sem, piece_sem, x_sem, in_sem, y1_ss, y1_rs, p1_ss, p1_rs, y2_ss, y2_rs, z_ss, z_rs, g2_ss, g2_rs, g1_ss, g1_rs,
     dp_ss, dp_rs, d_ss, d_rs, c_ss, c_rs, f2_ss, f2_rs, fw_ss, fw_rs,
 ):
     r = lax.axis_index("rep")
@@ -89,6 +89,12 @@
 
     x_copy = pltpu.make_async_copy(feat, x_s, x_sem)
     x_copy.start()
+    small = [
+        pltpu.make_async_copy(src, dst, in_sem.at[n])
+        for n, (src, dst) in enumerate(((w1_h, w1), (w2_h, w2), (lab_h, lab), (msk_h, msk)))
+    ]
+    for copy in small:
+        copy.start()
     rows_copy(0, 0).start()
 
     barrier = pltpu.get_barrier_semaphore()
@@ -96,6 +102,8 @@
     pl.semaphore_signal(barrier, inc=1, device_id=(nby, i), device_id_type=MESH)
     pl.semaphore_signal(barrier, inc=1, device_id=(r, other), device_id_type=MESH)
 
+    for copy in small:
+        copy.wait()
     w2n[...] = jnp.zeros_like(w2n)
     w2n[0:n_class, :] = w2[...]
     w2t = w2n[...].astype(BF)
@@ -507,10 +515,12 @@
     keep = pltpu.make_async_copy(fs.at[2, 1], dw1_o.at[i], x_sem)
     keep.start()
     f2_copy(2).wait_recv()
-    f_sum = f2[2] + f2r[2]
-    dw2_o[...] = f_sum[0:n_class]
-    loss_o[...] = f_sum[CP:CP + 1, 0:1] / count
+    rest[0:CP] = f2[2, 0:CP] + f2r[2, 0:CP]
+    rest[CP:CP + 8] = (f2[2, CP:CP + 8] + f2r[2, CP:CP + 8]) / count
+    rest_copy = pltpu.make_async_copy(rest, rest_o, in_sem.at[0])
+    rest_copy.start()
     keep.wait()
+    rest_copy.wait()
     back_recv().wait_recv()
 
     @pl.loop(0, 4)
@@ -540,9 +550,9 @@
     back().wait_send()
 
 
-def emit(loss, dw1, dw2, loss_o, dw1_o, dw2_o):
-    loss_o[...] = loss[...]
-    dw2_o[...] = dw2[...]
+def emit(dw1, rest, loss_o, dw1_o, dw2_o):
+    loss_o[...] = rest[CP:CP + 1, 0:1]
+    dw2_o[...] = rest[:dw2_o.shape[0]]
     dw1_o[:HR] = dw1[0]
     dw1_o[HR:] = dw1[1, :dw1_o.shape[0] - HR]
 
@@ -562,13 +572,17 @@
         sums = pl.pallas_call(
             body,
             out_shape=(
-                jax.ShapeDtypeStruct((1, 1), F32),
                 jax.ShapeDtypeStruct((2, HR, n_hid), F32),
-                jax.ShapeDtypeStruct((n_class, n_hid), F32),
+                jax.ShapeDtypeStruct((CP + 8, n_hid), F32),
             ),
-            in_specs=[hbm, hbm, vmem, vmem, vmem, vmem],
-            out_specs=(vmem, hbm, vmem),
+            in_specs=[hbm] * 6,
+            out_specs=(hbm, hbm),
             scratch_shapes=[
+                pltpu.VMEM((n_in, HID), F32),
+                pltpu.VMEM((n_class, HID), F32),
+                pltpu.VMEM((ND // HID, HID), jnp.int32),
+                pltpu.VMEM((ND // HID, HID), jnp.int32),
+                pltpu.VMEM((CP + 8, HID), F32),
                 pltpu.VMEM((4, 4, CH, NCOL), BF),
                 pltpu.VMEM((n_in, ND), BF),
                 pltpu.VMEM((CP, HID), F32),
@@ -594,7 +608,7 @@
                 pltpu.VMEM((3, 2, HR, HID), F32),
                 pltpu.VMEM((2, HR, HID), F32),
                 pltpu.VMEM((1, CH), F32),
-                dma((4,)), dma((2, NCH)), dma(()),
+                dma((4,)), dma((2, NCH)), dma(()), dma((4,)),
                 *[
                     dma(n) for n in ((4,), per, (NCH,), per, per, per, (NCH // 2,), (), (3,), (3,), (6,))
                     for _ in ("send", "receive")
@@ -611,7 +625,7 @@
                 jax.ShapeDtypeStruct((n_in, n_hid), F32),
                 jax.ShapeDtypeStruct((n_class, n_hid), F32),
             ),
-            in_specs=[vmem] * 3,
+            in_specs=[vmem] * 2,
             out_specs=(vmem, vmem, vmem),
         )(*sums)
         return loss.reshape(()), dw1, dw2.T

time: 124 us -> 122 us (0.984)
  Pallas kernels: 123 us -> 121 us
    pallas_call x1, Pallas kernels: 121 us -> 120 us  [device_step(): pl.pallas_call(body, out_shape=(jax.ShapeDtypeStruct((2, HR, n_hid), F32)...]
where the time goes in v4:
time: 122 us
  Pallas kernels  121 us (99%)
    pallas_call x1, Pallas kernels, device_step(): pl.pallas_call(body, out_shape=(jax.ShapeDtypeStruct((2, HR, n_hid), F32)...  120 us

profile of v4, /device:TPU:0, one launch (start us, length us, event | category | flops | bytes accessed | tf_op | source)
XLA Modules:
  0.0 121.9 jit_solution(18030285818087136077)
XLA Ops:
  0.6 119.5 %shard_map.85 = (f32[2,304,128]{2,1,0:T(8,128)}, f32[56,128]{1,0:T(8,128)}) custom-call(bf16[4,2048,4096]{2,1,0:T(8,128)(2,1)} %refs_0_.1, bf16[602,2048]{1,0:T(8,128)(2,1)} %bitcast.6, f32[602,128]{1,0:T(8,128)} %refs_2_.1, f32[41,128]{1,0:T(8,128)} %bitcast.7, s32[16,128]{1,0:T(8,128)} %bitcast.8, s32[16,128]{1,0:T(8,128)} %bitcast.9), custom_call_target="tpu_custom_call" | custom-call | tf_op jit(solution)/shard_map/pallas_call | solution.py:572
  120.2 1.7 %shard_map.86 = (f32[1,1]{1,0:T(1,128)}, f32[602,128]{1,0:T(8,128)}, f32[41,128]{1,0:T(8,128)}) custom-call(f32[2,304,128]{2,1,0:T(8,128)} %get-tuple-element.8.dw1, f32[56,128]{1,0:T(8,128)} %get-tuple-element.9.rest), custom_call_target="tpu_custom_call" | custom-call | tf_op jit(solution)/shard_map/pallas_call | solution.py:621

commit v5 on v4

--- a/solution.py
+++ b/solution.py
@@ -24,7 +24,7 @@
 M1, M2, M3, M4 = LAGS2
 N1, N2, N3 = LAGS3
 LN = 1
-LZ = 1
+LZ = 0
 LG = 1
 LB = 1
 NROW = 4

time: 122 us -> 122 us (level)
  no operation moved by 1% of the time
where the time goes in v5:
time: 122 us
  Pallas kernels  121 us (99%)
    pallas_call x1, Pallas kernels, device_step(): pl.pallas_call(body, out_shape=(jax.ShapeDtypeStruct((2, HR, n_hid), F32)...  119 us

profile of v5, /device:TPU:0, one launch (start us, length us, event | category | flops | bytes accessed | tf_op | source)
XLA Modules:
  0.0 121.7 jit_solution(5240803562282658047)
XLA Ops:
  0.6 119.3 %shard_map.85 = (f32[2,304,128]{2,1,0:T(8,128)}, f32[56,128]{1,0:T(8,128)}) custom-call(bf16[4,2048,4096]{2,1,0:T(8,128)(2,1)} %refs_0_.1, bf16[602,2048]{1,0:T(8,128)(2,1)} %bitcast.6, f32[602,128]{1,0:T(8,128)} %refs_2_.1, f32[41,128]{1,0:T(8,128)} %bitcast.7, s32[16,128]{1,0:T(8,128)} %bitcast.8, s32[16,128]{1,0:T(8,128)} %bitcast.9), custom_call_target="tpu_custom_call" | custom-call | tf_op jit(solution)/shard_map/pallas_call | solution.py:572
  120.0 1.7 %shard_map.86 = (f32[1,1]{1,0:T(1,128)}, f32[602,128]{1,0:T(8,128)}, f32[41,128]{1,0:T(8,128)}) custom-call(f32[2,304,128]{2,1,0:T(8,128)} %get-tuple-element.8.dw1, f32[56,128]{1,0:T(8,128)} %get-tuple-element.9.rest), custom_call_target="tpu_custom_call" | custom-call | tf_op jit(solution)/shard_map/pallas_call | solution.py:621
